TPU v7x, 32 devices: a whole 2x2x4 slice. The times are simulated.
32 devices in a mesh: row: 4 (over y, x), col: 8 (over z, core).
Axes of the slice: x: 2, y: 2, z: 4, core: 2. Of those that a mesh axis runs over, the one named last changes fastest.
Arguments:
- features: bfloat16 [32, 512, 768], P('row', 'col'), may hold values from -6 to 6
- norm_scale: float32 [768], replicated, may hold values from 0.5 to 1.5
- norm_shift: float32 [768], replicated, may hold values from -3 to 3
- expand_weight: bfloat16 [768, 3072], replicated, may hold values from -0.21875 to 0.21875
- expand_bias: float32 [3072], replicated, may hold values from -3 to 3
- depth_kernel: float32 [3, 3, 3072], replicated, may hold values from -2 to 2
- depth_bias: float32 [3072], replicated, may hold values from -3 to 3
- project_weight: bfloat16 [3072, 768], replicated, may hold values from -0.109375 to 0.109375
- project_bias: float32 [768], replicated, may hold values from -2 to 2
- attn_gain: float32 [768], replicated, may hold values from 0.25 to 1.75
- attn_shift: float32 [768], replicated, may hold values from -2 to 2
- qkv_weight: bfloat16 [768, 2304], replicated, may hold values from -0.21875 to 0.21875
- qkv_bias: float32 [2304], replicated, may hold values from -2 to 2
- out_weight: bfloat16 [768, 768], replicated, may hold values from -0.21875 to 0.21875
- out_bias: float32 [768], replicated, may hold values from -2 to 2
Outputs:
- output: bfloat16 [32, 512, 768], P('row', 'col')
All inputs are finite; a program needn't handle non-finite values.
Results may differ from a plain program's by a relative error of at most 0.006.
Values may be sent and summed in bfloat16 or wider, within the bound.
No kernel may reach another device: no remote copies, remote signals or barrier semaphores. Data moves between devices by JAX's collectives and lax.ppermute only.
A program may use at most 192 MiB of HBM per device.

v0:
```python
import math

import jax
import jax.numpy as jnp
from jax import lax
from jax.sharding import PartitionSpec as P

HEADS = 24
HEAD_DIM = 32
GRID = 8


def extended(cells, sides, width):
    for axis, dim in sides:
        count = lax.axis_size(axis)
        ends = count - 1
        head = lax.slice_in_dim(cells, 0, width, axis=dim)
        tail = lax.slice_in_dim(cells, cells.shape[dim] - width, cells.shape[dim], axis=dim)
        cells = jnp.concatenate(
            [
                lax.ppermute(tail, axis, [(i, (i + 1) % count) for i in range(ends)]),
                cells,
                lax.ppermute(head, axis, [((i + 1) % count, i) for i in range(ends)]),
            ],
            axis=dim,
        )
    return cells


def expand_cells(inputs, norm_scale, norm_shift, expand_weight, expand_bias):
    normed = (inputs.astype(jnp.float32) * norm_scale + norm_shift).astype(jnp.bfloat16)
    flat_rows = normed.reshape(-1, normed.shape[-1])
    hidden = jax.nn.gelu(
        jnp.dot(flat_rows, expand_weight, preferred_element_type=jnp.float32) + expand_bias
    )
    return hidden.astype(jnp.bfloat16).reshape(inputs.shape[:-1] + (expand_weight.shape[1],))


def layer_norm(values, scale_vec, shift_vec):
    widened = values.astype(jnp.float32)
    center = widened - jnp.mean(widened, axis=-1, keepdims=True)
    spread = jnp.mean(center * center, axis=-1, keepdims=True)
    return (center * lax.rsqrt(spread + 1e-06) * scale_vec + shift_vec).astype(jnp.bfloat16)


def attend(tokens_in, pattern, qkv_weight, qkv_bias, out_weight, out_bias):
    channels = tokens_in.shape[-1]
    leading = tokens_in.shape[:-1]
    projected = (
        jnp.dot(tokens_in.reshape(-1, channels), qkv_weight, preferred_element_type=jnp.float32)
        + qkv_bias
    )
    projected = projected.astype(jnp.bfloat16).reshape(leading + (3, HEADS, HEAD_DIM))
    query_part = projected[..., 0, :, :]
    key_part = projected[..., 1, :, :]
    value_part = projected[..., 2, :, :]
    renamed = {"i": "m", "j": "n", "k": "o", "l": "p"}
    token_letters = "ijkl"
    key_pattern = "".join((renamed.get(letter, letter) for letter in pattern))
    groups = "".join((letter for letter in pattern if letter not in token_letters))
    query_tokens = "".join((letter for letter in pattern if letter in token_letters))
    key_tokens = "".join((renamed[letter] for letter in query_tokens))
    score_form = groups + "h" + query_tokens + key_tokens
    scores = jnp.einsum(
        pattern + "hd," + key_pattern + "hd->" + score_form,
        query_part,
        key_part,
        preferred_element_type=jnp.float32,
    ) * (1.0 / math.sqrt(HEAD_DIM))
    weights = jnp.exp(scores)
    total = jnp.sum(weights, axis=tuple(range(-len(key_tokens), 0)), keepdims=True)
    probs = (weights / total).astype(jnp.bfloat16)
    mixed = jnp.einsum(
        score_form + "," + key_pattern + "hd->" + pattern + "hd",
        probs,
        value_part,
        preferred_element_type=jnp.float32,
    )
    mixed = mixed.astype(jnp.bfloat16)
    result = (
        jnp.dot(mixed.reshape(-1, channels), out_weight, preferred_element_type=jnp.float32)
        + out_bias
    )
    return result.astype(jnp.bfloat16).reshape(tokens_in.shape)


def per_device(
    features,
    norm_scale,
    norm_shift,
    expand_weight,
    expand_bias,
    depth_kernel,
    depth_bias,
    project_weight,
    project_bias,
    attn_gain,
    attn_shift,
    qkv_weight,
    qkv_bias,
    out_weight,
    out_bias,
):
    tile_rows, tile_cols, channels = features.shape
    row_count = lax.axis_size("row")
    col_count = lax.axis_size("col")
    hidden = expand_cells(features, norm_scale, norm_shift, expand_weight, expand_bias)
    padded = extended(hidden, (("row", 0), ("col", 1)), 1)
    summed = jnp.zeros((tile_rows, tile_cols, padded.shape[-1]), jnp.float32)
    for row_off in range(3):
        for col_off in range(3):
            summed = (
                summed
                + padded[row_off : row_off + tile_rows, col_off : col_off + tile_cols].astype(
                    jnp.float32
                )
                * depth_kernel[row_off, col_off]
            )
    depthwise = jax.nn.gelu(summed + depth_bias).astype(jnp.bfloat16)
    projected = (
        jnp.dot(
            depthwise.reshape(-1, depthwise.shape[-1]),
            project_weight,
            preferred_element_type=jnp.float32,
        )
        + project_bias
    )
    after_conv = (
        features.astype(jnp.float32) + projected.reshape(tile_rows, tile_cols, channels)
    ).astype(jnp.bfloat16)
    attn_in = layer_norm(after_conv, attn_gain, attn_shift)
    fold_row = max(1, GRID // row_count)
    fold_col = max(1, GRID // col_count)
    parity_row = max(1, row_count // GRID)
    parity_col = max(1, col_count // GRID)
    block_row = tile_rows // (fold_row * row_count)
    block_col = tile_cols // (fold_col * col_count)
    tile_view = attn_in.reshape(
        fold_row, row_count, block_row, fold_col, col_count, block_col, channels
    )
    ordered = tile_view.transpose(1, 4, 0, 2, 3, 5, 6).reshape(
        row_count * col_count, fold_row, block_row, fold_col, block_col, channels
    )
    received = lax.all_to_all(ordered, ("row", "col"), split_axis=0, concat_axis=0, tiled=True)
    item_count = received.shape[2]
    grouped = received.reshape(
        row_count // parity_row,
        parity_row,
        col_count // parity_col,
        parity_col,
        fold_row,
        item_count,
        fold_col,
        block_col,
        channels,
    )
    answered = attend(grouped, "jelfiukv", qkv_weight, qkv_bias, out_weight, out_bias).reshape(
        received.shape
    )
    returned = lax.all_to_all(answered, ("row", "col"), split_axis=0, concat_axis=0, tiled=True)
    returned_tiles = returned.reshape(
        row_count, col_count, fold_row, block_row, fold_col, block_col, channels
    ).transpose(2, 0, 3, 4, 1, 5, 6)
    attended = returned_tiles.reshape(tile_rows, tile_cols, channels)
    return (after_conv.astype(jnp.float32) + attended.astype(jnp.float32)).astype(jnp.bfloat16)


def solution(mesh):
    return jax.shard_map(
        per_device,
        mesh=mesh,
        in_specs=(
            P("row", "col", None),
            P(),
            P(),
            P(),
            P(),
            P(),
            P(),
            P(),
            P(),
            P(),
            P(),
            P(),
            P(),
            P(),
            P(),
        ),
        out_specs=P("row", "col", None),
        check_vma=False,
    )
```

profile of v0, /device:TPU:0, one launch (start us, length us, event | category | flops | bytes accessed | tf_op | source)
XLA Modules:
  0.0 190.2 jit_solution(3454715403288930277)
XLA Ops:
  0.0 1.5 fusion.31
  1.5 6.6 %fusion.10 = bf16[512,3072]{1,0:T(8,128)(2,1)S(1)} fusion(bf16[512,768]{1,0:T(8,128)(2,1)S(1)} %bitcast.90, bf16[768,3072]{1,0:T(8,128)(2,1)} %param.18, f32[3072]{0:T(1024)} %param.19), kind=kOutput, calls=%fused_computation.14 | convolution fusion | flops 2431647744 | bytes 8663040 | tf_op jit(solution)/shard_map/dot_general | solution.py:34
  8.2 4.9 %collective-permute-start = (bf16[1,64,3072]{2,1,0:T(8,128)(2,1)S(1)}, bf16[1,64,3072]{2,1,0:T(8,128)(2,1)S(1)}, u32[]{:S(2)}, u32[]{:S(2)}) collective-permute-start(bf16[1,64,3072]{2,1,0:T(8,128)(2,1)S(1)} %get-tuple-element.14), channel_id=1, source_target_pairs={{0,8},{8,16},{16,24},{1,9},{9,17},{17,25},{2,10},{10,18},{18,26},{... | collective-permute-start | bytes 1179656 | tf_op jit(solution)/shard_map/ppermute | solution.py:21
  13.1 1.3 collective-permute-start.1
  14.4 7.0 %collective-permute-done = bf16[1,64,3072]{2,1,0:T(8,128)(2,1)S(1)} collective-permute-done((bf16[1,64,3072]{2,1,0:T(8,128)(2,1)S(1)}, bf16[1,64,3072]{2,1,0:T(8,128)(2,1)S(1)}, u32[]{:S(2)}, u32[]{:S(2)}) %collective-permute-start) | collective-permute-done | bytes 393248 | tf_op jit(solution)/shard_map/ppermute | solution.py:21
  21.4 10.4 %collective-permute-done.1 = bf16[1,64,3072]{2,1,0:T(8,128)(2,1)S(1)} collective-permute-done((bf16[1,64,3072]{2,1,0:T(8,128)(2,1)S(1)}, bf16[1,64,3072]{2,1,0:T(8,128)(2,1)S(1)}, u32[]{:S(2)}, u32[]{:S(2)}) %collective-permute-start.1) | collective-permute-done | bytes 393248 | tf_op jit(solution)/shard_map/ppermute | solution.py:23
  32.0 1.3 collective-permute-start.2
  33.3 1.3 collective-permute-start.3
  34.7 3.6 %collective-permute-done.3 = bf16[10,1,3072]{2,1,0:T(2,128)(2,1)S(1)} collective-permute-done((bf16[10,1,3072]{2,1,0:T(2,128)(2,1)S(1)}, bf16[10,1,3072]{2,1,0:T(2,128)(2,1)S(1)}, u32[]{:S(2)}, u32[]{:S(2)}) %collective-permute-start.3) | collective-permute-done | bytes 61472 | tf_op jit(solution)/shard_map/ppermute | solution.py:23
  38.4 2.3 %maximum_maximum_fusion = (bf16[10,65,3072]{2,1,0:T(8,128)(2,1)S(1)}, bf16[10,65,3072]{2,1,0:T(8,128)(2,1)S(1)}) fusion(bf16[1,64,3072]{2,1,0:T(8,128)(2,1)S(1)} %collective-permute-done.1, bf16[8,64,3072]{2,1,0:T(8,128)(2,1)S(1)} %bitcast.80, bf16[1,64,3072]{2,1,0:T(8,128)(2,1)S(1)} %collective-permute-done, ...), kind=kLoop, calls=%fused_computation.26 | loop fusion | flops 31948800 | bytes 12042240 | tf_op jit(solution)/shard_map/concatenate | solution.py:19
  40.7 9.6 %fusion.18 = bf16[8,64,3072]{2,1,0:T(8,128)(2,1)S(1)} fusion(bf16[8,64,3072]{2,1,0:T(8,128)(2,1)S(1)} %bitcast.81, bf16[10,65,3072]{2,1,0:T(8,128)(2,1)S(1)} %get-tuple-element.11, bf16[1,64,3072]{2,1,0:T(8,128)(2,1)S(1)} %collective-permute-done.1, bf16[10,65,3072]{2,1,0:T(8,128)(2,1)S(1)} %get-tuple-element.10, ...), kind=kLoop, calls=%fused_computation.22 | loop fusion | flops 59768832 | bytes 26075136 | tf_op jit(solution)/shard_map/convert_element_type | solution.py:119
  50.4 2.6 %convolution_add_fusion.1 = f32[512,768]{1,0:T(8,128)S(1)} fusion(bf16[512,3072]{1,0:T(8,128)(2,1)S(1)} %bitcast.86, bf16[3072,768]{1,0:T(8,128)(2,1)S(1)} %bitcast.101, f32[768]{0:T(1024)S(1)} %copy-done.10), kind=kOutput, calls=%fused_computation.52 | convolution fusion | flops 2416312320 | bytes 9440256 | tf_op jit(solution)/shard_map/dot_general | solution.py:121
  53.7 0.5 copy-done.2
  54.6 28.6 %all_to_all.10 = bf16[32,2,1,1,8,768]{5,4,1,3,2,0:T(8,128)(2,1)S(1)} all-to-all(bf16[32,2,1,1,8,768]{5,4,1,3,2,0:T(8,128)(2,1)S(1)} %bitcast.84), channel_id=1, replica_groups=mesh['row'=4,'col'=8] {'row','col'}, dimensions={0} | all-to-all | bytes 1572864 | tf_op jit(solution)/shard_map/all_to_all | solution.py:144
  83.3 3.4 %fusion.19 = bf16[512,2304]{1,0:T(8,128)(2,1)} fusion(bf16[512,768]{1,0:T(8,128)(2,1)S(1)} %bitcast.88, bf16[768,2304]{1,0:T(8,128)(2,1)S(1)} %copy-done, f32[2304]{0:T(1024)S(1)} %copy-done.9), kind=kOutput, calls=%fused_computation.25 | convolution fusion | flops 1814298624 | bytes 6693888 | tf_op jit(solution)/shard_map/dot_general | solution.py:50
  86.7 11.6 %reshape.85 = bf16[4,1,8,1,2,1,1,8,3,24,32]{10,9,8,7,4,2,0,6,5,3,1:T(8,128)(2,1)} reshape(bf16[512,2304]{1,0:T(8,128)(2,1)} %fusion.19) | data formatting | bytes 4718592 | tf_op jit(solution)/shard_map/reshape | solution.py:53
  98.2 6.3 %fusion.35 = (bf16[4,1,8,1,2,1,1,8,1,24,32]{10,9,8,7,4,2,0,6,5,3,1:T(8,128)(2,1)}, bf16[4,1,8,1,2,1,1,8,1,24,32]{10,9,8,7,4,2,0,6,5,3,1:T(8,128)(2,1)S(1)}, bf16[4,1,8,1,2,1,1,8,1,24,32]{10,9,8,7,4,2,0,6,5,3,1:T(8,128)(2,1)S(1)}) fusion(bf16[4,1,8,1,2,1,1,8,3,24,32]{10,9,8,7,4,2,0,6,5,3,1:T(8,128)(2,1)} %reshape.85), kind=kLoop, calls=%fused_computation.60 | loop fusion | bytes 4718592 | tf_op jit(solution)/shard_map/slice | solution.py:56
  104.5 27.2 %fusion = (f32[8,24,4,8,2]{3,4,2,1,0:T(2,128)}, f32[8,24,4,8,2,4,8,2]{3,6,7,5,4,2,1,0:T(8,128)}) fusion(bf16[4,1,8,1,2,1,1,8,1,24,32]{10,9,8,7,4,2,0,6,5,3,1:T(8,128)(2,1)S(1)} %get-tuple-element.8, bf16[4,1,8,1,2,1,1,8,1,24,32]{10,9,8,7,4,2,0,6,5,3,1:T(8,128)(2,1)S(1)} %get-tuple-element.9), kind=kOutput, calls=%fused_computation.2 | convolution fusion | flops 51892224 | bytes 4767744 | tf_op jit(solution)/shard_map/jelfiukvhd,nepfmuovhd->efuvhjliknpmo/dot_general | solution.py:64
  131.7 24.1 %fusion.20 = bf16[4,1,8,1,2,1,1,8,24,32]{9,2,4,0,8,7,6,5,3,1:T(8,128)(2,1)} fusion(bf16[4,1,8,1,2,1,1,8,1,24,32]{10,9,8,7,4,2,0,6,5,3,1:T(8,128)(2,1)} %get-tuple-element.7, f32[8,24,4,8,2,4,8,2]{3,6,7,5,4,2,1,0:T(8,128)} %get-tuple-element.26, f32[8,24,4,8,2]{3,4,2,1,0:T(2,128)} %get-tuple-element.25), kind=kOutput, calls=%fused_computation.28 | convolution fusion | flops 53084160 | bytes 4767744 | tf_op jit(solution)/shard_map/efuvhjliknpmo,nepfmuovhd->jelfiukvhd/dot_general | solution.py:73
  155.7 3.9 %copy.33 = bf16[4,1,8,1,2,1,1,8,24,32]{9,8,7,4,2,0,6,5,3,1:T(8,128)(2,1)S(1)} copy(bf16[4,1,8,1,2,1,1,8,24,32]{9,2,4,0,8,7,6,5,3,1:T(8,128)(2,1)} %fusion.20) | data formatting | bytes 1572864 | tf_op jit(solution)/shard_map/convert_element_type | solution.py:79
  159.7 2.8 %reshape.89 = bf16[512,768]{1,0:T(8,128)(2,1)} reshape(bf16[4,1,8,1,2,1,1,8,24,32]{9,8,7,4,2,0,6,5,3,1:T(8,128)(2,1)S(1)} %copy.33) | data formatting | bytes 1572864 | tf_op jit(solution)/shard_map/reshape | solution.py:81
  162.5 2.4 %add_convert_fusion = bf16[512,768]{1,0:T(8,128)(2,1)S(1)} fusion(bf16[512,768]{1,0:T(8,128)(2,1)} %reshape.89, bf16[768,768]{1,0:T(8,128)(2,1)} %param.28, f32[768]{0:T(1024)S(1)} %copy-done.11), kind=kOutput, calls=%fused_computation.51 | convolution fusion | flops 604766208 | bytes 2755584 | tf_op jit(solution)/shard_map/dot_general | solution.py:81
  164.9 24.0 %all_to_all.11 = bf16[32,2,1,1,8,768]{5,4,1,3,2,0:T(8,128)(2,1)S(1)} all-to-all(bf16[32,2,1,1,8,768]{5,4,1,3,2,0:T(8,128)(2,1)S(1)} %bitcast.89), channel_id=1, replica_groups=mesh['row'=4,'col'=8] {'row','col'}, dimensions={0} | all-to-all | bytes 1572864 | tf_op jit(solution)/shard_map/all_to_all | solution.py:160
  189.1 1.1 fusion.33
  (40 shorter events, 1.7 us)
Async XLA Ops:
  0.0 83.2 %copy-start = (bf16[768,2304]{1,0:T(8,128)(2,1)S(1)}, bf16[768,2304]{1,0:T(8,128)(2,1)}, u32[]{:S(2)}) copy-start(bf16[768,2304]{1,0:T(8,128)(2,1)} %param.26) | copy-start | bytes 10616836
  8.1 26.5 %copy-start.5 = (f32[3,3,3072]{2,1,0:T(4,128)S(1)}, f32[3,3,3072]{2,1,0:T(4,128)}, u32[]{:S(2)}) copy-start(f32[3,3,3072]{2,1,0:T(4,128)} %param.20) | copy-start | bytes 331780
  8.2 13.2 %collective-permute-start = (bf16[1,64,3072]{2,1,0:T(8,128)(2,1)S(1)}, bf16[1,64,3072]{2,1,0:T(8,128)(2,1)S(1)}, u32[]{:S(2)}, u32[]{:S(2)}) collective-permute-start(bf16[1,64,3072]{2,1,0:T(8,128)(2,1)S(1)} %get-tuple-element.14), channel_id=1, source_target_pairs={{0,8},{8,16},{16,24},{1,9},{9,17},{17,25},{2,10},{10,18},{18,26},{... | collective-permute-start | bytes 1179656 | tf_op jit(solution)/shard_map/ppermute | solution.py:21
  13.1 18.7 %collective-permute-start.1 = (bf16[1,64,3072]{2,1,0:T(8,128)(2,1)S(1)}, bf16[1,64,3072]{2,1,0:T(8,128)(2,1)S(1)}, u32[]{:S(2)}, u32[]{:S(2)}) collective-permute-start(bf16[1,64,3072]{2,1,0:T(8,128)(2,1)S(1)} %get-tuple-element.15), channel_id=1, source_target_pairs={{8,0},{16,8},{24,16},{9,1},{17,9},{25,17},{10,2},{18,10},{26,18},{... | collective-permute-start | bytes 1179656 | tf_op jit(solution)/shard_map/ppermute | solution.py:23
  32.0 2.7 %collective-permute-start.2 = (bf16[10,1,3072]{2,1,0:T(2,128)(2,1)S(1)}, bf16[10,1,3072]{2,1,0:T(2,128)(2,1)S(1)}, u32[]{:S(2)}, u32[]{:S(2)}) collective-permute-start(bf16[10,1,3072]{2,1,0:T(2,128)(2,1)S(1)} %get-tuple-element.12), channel_id=1, source_target_pairs={{0,1},{1,2},{2,3},{3,4},{4,5},{5,6},{6,7},{8,9},{9,10},{10,11},{11... | collective-permute-start | bytes 184328 | tf_op jit(solution)/shard_map/ppermute | solution.py:21
  33.3 5.0 %collective-permute-start.3 = (bf16[10,1,3072]{2,1,0:T(2,128)(2,1)S(1)}, bf16[10,1,3072]{2,1,0:T(2,128)(2,1)S(1)}, u32[]{:S(2)}, u32[]{:S(2)}) collective-permute-start(bf16[10,1,3072]{2,1,0:T(2,128)(2,1)S(1)} %get-tuple-element.13), channel_id=1, source_target_pairs={{1,0},{2,1},{3,2},{4,3},{5,4},{6,5},{7,6},{9,8},{10,9},{11,10},{12... | collective-permute-start | bytes 184328 | tf_op jit(solution)/shard_map/ppermute | solution.py:23
  34.7 5.9 %copy-start.6 = (f32[3072]{0:T(1024)S(1)}, f32[3072]{0:T(1024)}, u32[]{:S(2)}) copy-start(f32[3072]{0:T(1024)} %param.21) | copy-start | bytes 36868
  38.4 12.0 %slice-start = ((s8[4718592]{0:T(1024)(128)(4,1)}), s8[4194304]{0:T(1024)(128)(4,1)S(1)}, s32[]{:S(2)}) async-start(s8[4718592]{0:T(1024)(128)(4,1)} %bitcast.100), calls=%async_computation.2 | async-start | bytes 8388608
  40.7 9.7 %slice-start.1 = ((s8[4718592]{0:T(1024)(128)(4,1)}), s8[524288]{0:T(1024)(128)(4,1)S(1)}, s32[]{:S(2)}) async-start(s8[4718592]{0:T(1024)(128)(4,1)} %bitcast.100), calls=%async_computation.3 | async-start | bytes 1048576
  40.7 9.7 %copy-start.10 = (f32[768]{0:T(1024)S(1)}, f32[768]{0:T(1024)}, u32[]{:S(2)}) copy-start(f32[768]{0:T(1024)} %param.23) | copy-start | bytes 9220
  50.4 2.7 %copy-start.4 = (bf16[8,64,768]{2,1,0:T(8,128)(2,1)S(1)}, bf16[8,64,768]{2,1,0:T(8,128)(2,1)}, u32[]{:S(2)}) copy-start(bf16[8,64,768]{2,1,0:T(8,128)(2,1)} %param.15) | copy-start | bytes 2359300
  50.4 3.8 %copy-start.7 = (f32[768]{0:T(1024)S(1)}, f32[768]{0:T(1024)}, u32[]{:S(2)}) copy-start(f32[768]{0:T(1024)} %param.25) | copy-start | bytes 9220
  50.4 3.8 %copy-start.8 = (f32[768]{0:T(1024)S(1)}, f32[768]{0:T(1024)}, u32[]{:S(2)}) copy-start(f32[768]{0:T(1024)} %param.24) | copy-start | bytes 9220
  53.0 30.2 %copy-start.9 = (f32[2304]{0:T(1024)S(1)}, f32[2304]{0:T(1024)}, u32[]{:S(2)}) copy-start(f32[2304]{0:T(1024)} %param.27) | copy-start | bytes 27652
  53.3 0.9 copy-start.2
  155.7 6.7 %copy-start.11 = (f32[768]{0:T(1024)S(1)}, f32[768]{0:T(1024)}, u32[]{:S(2)}) copy-start(f32[768]{0:T(1024)} %param.29) | copy-start | bytes 9220
  162.5 26.7 %copy-start.3 = (bf16[8,64,768]{2,1,0:T(8,128)(2,1)S(1)}, bf16[8,64,768]{2,1,0:T(8,128)(2,1)}, u32[]{:S(2)}) copy-start(bf16[8,64,768]{2,1,0:T(8,128)(2,1)} %copy-done.2) | copy-start | bytes 2359300
  164.8 25.4 %copy-start.1 = (bf16[768,2304]{1,0:T(8,128)(2,1)S(1)}, bf16[768,2304]{1,0:T(8,128)(2,1)}, u32[]{:S(2)}) copy-start(bf16[768,2304]{1,0:T(8,128)(2,1)} %param.26) | copy-start | bytes 10616836
where the time goes:
time: 191 us; the launch traced here: 190 us
  matrix products  66.3 us (35%)
  blocking collectives  52.6 us (28%)
  local copies, waits for them, and re-layouts  25.5 us (13%)
  waiting for transfers between devices  21 us (11%)
  other arithmetic  15.8 us (8%)
  starting transfers between devices  8.76 us (5%)
    all_to_all x1, blocking collectives, per_device(): lax.all_to_all(ordered, ('row', 'col'), split_axis=0, concat_axis=0, tile...  28.6 us
    dot_general x1, matrix products, attend(): jnp.einsum(pattern + 'hd,' + key_pattern + 'hd->' + score_form, query_par...  27.2 us
    dot_general x1, matrix products, attend(): jnp.einsum(score_form + ',' + key_pattern + 'hd->' + pattern + 'hd', prob...  24.1 us
    all_to_all x1, blocking collectives, per_device(): lax.all_to_all(answered, ('row', 'col'), split_axis=0, concat_axis=0, til...  24 us
    ppermute x2, waiting for transfers between devices, extended(): lax.ppermute(head, axis, [((i + 1) % count, i) for i in range(ends)])  14 us
    reshape x1, local copies, waits for them, and re-layouts, attend(): projected.astype(jnp.bfloat16).reshape(leading + (3, HEADS, HEAD_DIM))  11.6 us
    convert_element_type x1, other arithmetic, per_device(): depthwise = jax.nn.gelu(summed + depth_bias).astype(jnp.bfloat16)  9.63 us
    ppermute x2, waiting for transfers between devices, extended(): lax.ppermute(tail, axis, [(i, (i + 1) % count) for i in range(ends)])  7.04 us
  transfers between devices with their start and end apart: 4, of which 3 were waited for; matrix products, arithmetic and copies ran while one was open for 0% of the time, Pallas kernels for 0%

commit v1 on v0

--- a/solution.py
+++ b/solution.py
@@ -1,13 +1,19 @@
+import functools
 import math
 
 import jax
 import jax.numpy as jnp
+import numpy as np
 from jax import lax
+from jax.experimental import pallas as pl
+from jax.experimental.pallas import tpu as pltpu
 from jax.sharding import PartitionSpec as P
 
 HEADS = 24
 HEAD_DIM = 32
 GRID = 8
+LANES = 128
+PACK = LANES // HEAD_DIM
 
 
 def extended(cells, sides, width):
@@ -43,45 +49,104 @@
     return (center * lax.rsqrt(spread + 1e-06) * scale_vec + shift_vec).astype(jnp.bfloat16)
 
 
-def attend(tokens_in, pattern, qkv_weight, qkv_bias, out_weight, out_bias):
-    channels = tokens_in.shape[-1]
-    leading = tokens_in.shape[:-1]
-    projected = (
-        jnp.dot(tokens_in.reshape(-1, channels), qkv_weight, preferred_element_type=jnp.float32)
-        + qkv_bias
-    )
-    projected = projected.astype(jnp.bfloat16).reshape(leading + (3, HEADS, HEAD_DIM))
-    query_part = projected[..., 0, :, :]
-    key_part = projected[..., 1, :, :]
-    value_part = projected[..., 2, :, :]
-    renamed = {"i": "m", "j": "n", "k": "o", "l": "p"}
-    token_letters = "ijkl"
-    key_pattern = "".join((renamed.get(letter, letter) for letter in pattern))
-    groups = "".join((letter for letter in pattern if letter not in token_letters))
-    query_tokens = "".join((letter for letter in pattern if letter in token_letters))
-    key_tokens = "".join((renamed[letter] for letter in query_tokens))
-    score_form = groups + "h" + query_tokens + key_tokens
-    scores = jnp.einsum(
-        pattern + "hd," + key_pattern + "hd->" + score_form,
-        query_part,
-        key_part,
-        preferred_element_type=jnp.float32,
-    ) * (1.0 / math.sqrt(HEAD_DIM))
-    weights = jnp.exp(scores)
-    total = jnp.sum(weights, axis=tuple(range(-len(key_tokens), 0)), keepdims=True)
-    probs = (weights / total).astype(jnp.bfloat16)
-    mixed = jnp.einsum(
-        score_form + "," + key_pattern + "hd->" + pattern + "hd",
-        probs,
-        value_part,
-        preferred_element_type=jnp.float32,
-    )
-    mixed = mixed.astype(jnp.bfloat16)
-    result = (
-        jnp.dot(mixed.reshape(-1, channels), out_weight, preferred_element_type=jnp.float32)
-        + out_bias
-    )
-    return result.astype(jnp.bfloat16).reshape(tokens_in.shape)
+def attend_kernel(
+    group_size,
+    x_ref,
+    pick_ref,
+    place_ref,
+    qkv_weight_ref,
+    qkv_bias_ref,
+    out_weight_ref,
+    out_bias_ref,
+    o_ref,
+    qkv_ref,
+    mixed_ref,
+    probs_ref,
+):
+    count, channels = x_ref.shape
+    f32, bf16 = jnp.float32, jnp.bfloat16
+    half = count // 2
+    column = lax.broadcasted_iota(jnp.int32, (count, count), 1)
+    pick = (column == pick_ref[...]).astype(f32).astype(bf16)
+    x = jnp.dot(pick, x_ref[...], preferred_element_type=f32).astype(bf16)
+    step = 256
+    for lo in range(0, 3 * channels, step):
+        cols = slice(lo, lo + step)
+        part = jnp.dot(x, qkv_weight_ref[:, cols], preferred_element_type=f32)
+        qkv_ref[:, cols] = (part + qkv_bias_ref[:, cols]).astype(bf16)
+
+    wide = PACK * group_size
+    lane = lax.broadcasted_iota(jnp.int32, (wide, LANES), 1) // HEAD_DIM
+    row = lax.broadcasted_iota(jnp.int32, (wide, LANES), 0) // group_size
+    own = (lane == row).astype(f32).astype(bf16)
+    block_row = lax.broadcasted_iota(jnp.int32, (wide, wide), 0) // group_size
+    block_col = lax.broadcasted_iota(jnp.int32, (wide, wide), 1) // group_size
+    same = (block_row == block_col).astype(f32).astype(bf16)
+    scale = math.log2(math.e) / math.sqrt(HEAD_DIM)
+    top = float(jnp.finfo(bf16).max)
+    chunks = channels // LANES
+
+    def one_group(group, carry):
+        rows = pl.ds(pl.multiple_of(group * group_size, group_size), group_size)
+        for chunk in range(chunks):
+            lo = chunk * LANES
+            query = qkv_ref[rows, lo : lo + LANES]
+            key = qkv_ref[rows, channels + lo : channels + lo + LANES]
+            keys = jnp.concatenate([key] * PACK, axis=0) * own
+            scores = lax.dot_general(
+                query, keys, (((1,), (1,)), ((), ())), preferred_element_type=f32
+            )
+            probs_ref[chunk * group_size : (chunk + 1) * group_size, :] = jnp.exp2(scores * scale)
+        weights = probs_ref[...]
+        total = jnp.dot(jnp.minimum(weights, top).astype(bf16), same, preferred_element_type=f32)
+        probs = (weights / total).astype(bf16)
+        for chunk in range(chunks):
+            lo = chunk * LANES
+            value = qkv_ref[rows, 2 * channels + lo : 2 * channels + lo + LANES]
+            values = jnp.concatenate([value] * PACK, axis=0) * own
+            mixed_ref[rows, lo : lo + LANES] = jnp.dot(
+                probs[chunk * group_size : (chunk + 1) * group_size],
+                values,
+                preferred_element_type=f32,
+            ).astype(bf16)
+        return carry
+
+    lax.fori_loop(0, count // group_size, one_group, 0)
+    place = (column == place_ref[...]).astype(f32).astype(bf16)
+    result = jnp.dot(mixed_ref[...], out_weight_ref[...], preferred_element_type=f32)
+    result = (result + out_bias_ref[...]).astype(bf16)
+    o_ref[...] = jnp.dot(place, result, preferred_element_type=f32).astype(bf16)
+
+
+def attend(tokens, order, group_size, qkv_weight, qkv_bias, out_weight, out_bias):
+    count, channels = tokens.shape
+    pick = np.asarray(order, np.int32)
+    place = np.argsort(pick).astype(np.int32)
+    whole = pl.BlockSpec(memory_space=pltpu.VMEM)
+    return pl.pallas_call(
+        functools.partial(attend_kernel, group_size),
+        out_shape=jax.ShapeDtypeStruct((count, channels), jnp.bfloat16),
+        in_specs=[whole] * 7,
+        out_specs=whole,
+        scratch_shapes=[
+            pltpu.VMEM((count, 3 * channels), jnp.bfloat16),
+            pltpu.VMEM((count, channels), jnp.bfloat16),
+            pltpu.VMEM((channels // LANES * group_size, PACK * group_size), jnp.float32),
+        ],
+        cost_estimate=pl.CostEstimate(
+            flops=10 * count * channels * channels, bytes_accessed=8 << 20, transcendentals=1 << 20
+        ),
+        compiler_params=pltpu.CompilerParams(vmem_limit_bytes=40 << 20),
+        name="grid_attention",
+    )(
+        tokens,
+        jnp.asarray(pick)[:, None],
+        jnp.asarray(place)[:, None],
+        qkv_weight,
+        qkv_bias[None],
+        out_weight,
+        out_bias[None],
+    )
 
 
 def per_device(
@@ -104,8 +169,16 @@
     tile_rows, tile_cols, channels = features.shape
     row_count = lax.axis_size("row")
     col_count = lax.axis_size("col")
-    hidden = expand_cells(features, norm_scale, norm_shift, expand_weight, expand_bias)
-    padded = extended(hidden, (("row", 0), ("col", 1)), 1)
+    row_at = lax.axis_index("row")
+    col_at = lax.axis_index("col")
+    around = extended(features, (("row", 0), ("col", 1)), 1)
+    padded = expand_cells(around, norm_scale, norm_shift, expand_weight, expand_bias)
+    height = jnp.arange(tile_rows + 2) + row_at * tile_rows
+    width = jnp.arange(tile_cols + 2) + col_at * tile_cols
+    inside = ((height >= 1) & (height <= tile_rows * row_count))[:, None] & (
+        (width >= 1) & (width <= tile_cols * col_count)
+    )[None, :]
+    padded = jnp.where(inside[..., None], padded, 0)
     summed = jnp.zeros((tile_rows, tile_cols, padded.shape[-1]), jnp.float32)
     for row_off in range(3):
         for col_off in range(3):
@@ -142,21 +215,22 @@
         row_count * col_count, fold_row, block_row, fold_col, block_col, channels
     )
     received = lax.all_to_all(ordered, ("row", "col"), split_axis=0, concat_axis=0, tiled=True)
-    item_count = received.shape[2]
-    grouped = received.reshape(
+    tokens = received.reshape(-1, channels)
+    layout = np.arange(tokens.shape[0]).reshape(
         row_count // parity_row,
         parity_row,
         col_count // parity_col,
         parity_col,
         fold_row,
-        item_count,
+        block_row,
         fold_col,
         block_col,
-        channels,
-    )
-    answered = attend(grouped, "jelfiukv", qkv_weight, qkv_bias, out_weight, out_bias).reshape(
-        received.shape
-    )
+    )
+    order = layout.transpose(1, 3, 5, 7, 0, 2, 4, 6)
+    group_size = math.prod(order.shape[4:])
+    answered = attend(
+        tokens, order.reshape(-1), group_size, qkv_weight, qkv_bias, out_weight, out_bias
+    ).reshape(received.shape)
     returned = lax.all_to_all(answered, ("row", "col"), split_axis=0, concat_axis=0, tiled=True)
     returned_tiles = returned.reshape(
         row_count, col_count, fold_row, block_row, fold_col, block_col, channels
@@ -169,23 +243,7 @@
     return jax.shard_map(
         per_device,
         mesh=mesh,
-        in_specs=(
-            P("row", "col", None),
-            P(),
-            P(),
-            P(),
-            P(),
-            P(),
-            P(),
-            P(),
-            P(),
-            P(),
-            P(),
-            P(),
-            P(),
-            P(),
-            P(),
-        ),
+        in_specs=(P("row", "col", None),) + (P(),) * 14,
         out_specs=P("row", "col", None),
         check_vma=False,
     )

time: 191 us -> 117 us (0.61)
  matrix products: 66.3 us -> 12.6 us
  blocking collectives: 52.6 us -> 24 us
  local copies, waits for them, and re-layouts: 25.5 us -> 12.8 us
  Pallas kernels: 0 us -> 8.03 us
  starting transfers between devices: 8.76 us -> 15.9 us
  waiting for transfers between devices: 21 us -> 27.9 us
    dot_general x4 -> x0, matrix products: 57 us -> none  [the longest x1 27.2 us: attend(): jnp.einsum(pattern + 'hd,' + key_pattern + 'hd->' + score_form, query_par...]
    all_to_all x1 -> x0, blocking collectives: 28.6 us -> none  [per_device(): lax.all_to_all(ordered, ('row', 'col'), split_axis=0, concat_axis=0, tile...]
    all_to_all x0 -> x1, waiting for transfers between devices: none -> 21.6 us  [per_device(): lax.all_to_all(ordered, ('row', 'col'), split_axis=0, concat_axis=0, tile...]
    reshape x2 -> x1, local copies, waits for them, and re-layouts: 14.4 us -> 4.76 us  [expand_cells(): hidden.astype(jnp.bfloat16)]
    pallas_call x0 -> x1, Pallas kernels: none -> 8.03 us  [attend(): pl.pallas_call(functools.partial(attend_kernel, group_size), out_shape=ja...]
    ppermute x2, waiting for transfers between devices: 14 us -> 6.3 us  [extended(): lax.ppermute(head, axis, [((i + 1) % count, i) for i in range(ends)])]
    all_to_all x0 -> x1, starting transfers between devices: none -> 7.18 us  [per_device(): lax.all_to_all(ordered, ('row', 'col'), split_axis=0, concat_axis=0, tile...]
    ppermute x2, waiting for transfers between devices: 7.04 us -> 0.01 us  [extended(): lax.ppermute(tail, axis, [(i, (i + 1) % count) for i in range(ends)])]
  transfers between devices with their start and end apart: 4 -> 5, of which waited for: 3 -> 3; matrix products, arithmetic and copies ran while one was open for 0% -> 2% of each run, Pallas kernels for 0% -> 0%
where the time goes in v1:
time: 117 us; the launch traced here: 116 us
  waiting for transfers between devices  27.9 us (24%)
  blocking collectives  24 us (21%)
  starting transfers between devices  15.9 us (14%)
  other arithmetic  14.3 us (12%)
  local copies, waits for them, and re-layouts  12.8 us (11%)
  matrix products  12.6 us (11%)
  Pallas kernels  8.03 us (7%)
    all_to_all x1, blocking collectives, per_device(): lax.all_to_all(answered, ('row', 'col'), split_axis=0, concat_axis=0, til...  24 us
    all_to_all x1, waiting for transfers between devices, per_device(): lax.all_to_all(ordered, ('row', 'col'), split_axis=0, concat_axis=0, tile...  21.6 us
    dot_general x1, matrix products, expand_cells(): jnp.dot(flat_rows, expand_weight, preferred_element_type=jnp.float32)  10 us
    convert_element_type x1, other arithmetic, per_device(): depthwise = jax.nn.gelu(summed + depth_bias).astype(jnp.bfloat16)  8.95 us
    pallas_call x1, Pallas kernels, attend(): pl.pallas_call(functools.partial(attend_kernel, group_size), out_shape=ja...  8.03 us
    all_to_all x1, starting transfers between devices, per_device(): lax.all_to_all(ordered, ('row', 'col'), split_axis=0, concat_axis=0, tile...  7.18 us
    ppermute x2, waiting for transfers between devices, extended(): lax.ppermute(head, axis, [((i + 1) % count, i) for i in range(ends)])  6.3 us
    ppermute x2, starting transfers between devices, extended(): lax.ppermute(tail, axis, [(i, (i + 1) % count) for i in range(ends)])  6.17 us
  transfers between devices with their start and end apart: 5, of which 3 were waited for; matrix products, arithmetic and copies ran while one was open for 2% of the time, Pallas kernels for 0%

profile of v1, /device:TPU:0, one launch (start us, length us, event | category | flops | bytes accessed | tf_op | source)
XLA Modules:
  0.0 116.0 jit_solution(9098640329670125545)
XLA Ops:
  0.0 1.0 fusion.26
  1.0 4.9 %collective-permute-start = (bf16[1,64,768]{2,1,0:T(8,128)(2,1)S(1)}, bf16[1,64,768]{2,1,0:T(8,128)(2,1)S(1)}, u32[]{:S(2)}, u32[]{:S(2)}) collective-permute-start(bf16[1,64,768]{2,1,0:T(8,128)(2,1)S(1)} %get-tuple-element.10), channel_id=1, source_target_pairs={{0,8},{8,16},{16,24},{1,9},{9,17},{17,25},{2,10},{10,18},{18,26},{... | collective-permute-start | bytes 294920 | tf_op jit(solution)/shard_map/ppermute | solution.py:27
  5.8 1.3 %collective-permute-start.1 = (bf16[1,64,768]{2,1,0:T(8,128)(2,1)S(1)}, bf16[1,64,768]{2,1,0:T(8,128)(2,1)S(1)}, u32[]{:S(2)}, u32[]{:S(2)}) collective-permute-start(bf16[1,64,768]{2,1,0:T(8,128)(2,1)S(1)} %get-tuple-element.9), channel_id=1, source_target_pairs={{8,0},{16,8},{24,16},{9,1},{17,9},{25,17},{10,2},{18,10},{26,18},{... | collective-permute-start | bytes 294920 | tf_op jit(solution)/shard_map/ppermute | solution.py:29
  7.2 1.1 fusion.27
  8.4 1.2 %constant_dynamic-update-slice_fusion.1 = bf16[10,64,768]{2,1,0:T(8,128)(2,1)S(1)} fusion(bf16[10,64,768]{2,1,0:T(8,128)(2,1)S(1)} %constant_dynamic-update-slice_fusion.2, bf16[8,64,768]{2,1,0:T(8,128)(2,1)} %param.17), kind=kLoop, calls=%fused_computation.37 | loop fusion | bytes 1572864
  9.6 2.8 %collective-permute-done.1 = bf16[1,64,768]{2,1,0:T(8,128)(2,1)S(1)} collective-permute-done((bf16[1,64,768]{2,1,0:T(8,128)(2,1)S(1)}, bf16[1,64,768]{2,1,0:T(8,128)(2,1)S(1)}, u32[]{:S(2)}, u32[]{:S(2)}) %collective-permute-start.1) | collective-permute-done | bytes 98336 | tf_op jit(solution)/shard_map/ppermute | solution.py:29
  12.4 1.3 %collective-permute-start.2 = (bf16[10,1,768]{2,1,0:T(2,128)(2,1)S(1)}, bf16[10,1,768]{2,1,0:T(2,128)(2,1)S(1)}, u32[]{:S(2)}, u32[]{:S(2)}) collective-permute-start(bf16[10,1,768]{2,1,0:T(2,128)(2,1)S(1)} %get-tuple-element.7), channel_id=1, source_target_pairs={{0,1},{1,2},{2,3},{3,4},{4,5},{5,6},{6,7},{8,9},{9,10},{10,11},{11... | collective-permute-start | bytes 46088 | tf_op jit(solution)/shard_map/ppermute | solution.py:27
  13.7 1.3 %collective-permute-start.3 = (bf16[10,1,768]{2,1,0:T(2,128)(2,1)S(1)}, bf16[10,1,768]{2,1,0:T(2,128)(2,1)S(1)}, u32[]{:S(2)}, u32[]{:S(2)}) collective-permute-start(bf16[10,1,768]{2,1,0:T(2,128)(2,1)S(1)} %get-tuple-element.8), channel_id=1, source_target_pairs={{1,0},{2,1},{3,2},{4,3},{5,4},{6,5},{7,6},{9,8},{10,9},{11,10},{12... | collective-permute-start | bytes 46088 | tf_op jit(solution)/shard_map/ppermute | solution.py:29
  15.1 3.5 %collective-permute-done.3 = bf16[10,1,768]{2,1,0:T(2,128)(2,1)S(1)} collective-permute-done((bf16[10,1,768]{2,1,0:T(2,128)(2,1)S(1)}, bf16[10,1,768]{2,1,0:T(2,128)(2,1)S(1)}, u32[]{:S(2)}, u32[]{:S(2)}) %collective-permute-start.3) | collective-permute-done | bytes 15392 | tf_op jit(solution)/shard_map/ppermute | solution.py:29
  18.9 1.6 %reshape.98 = f32[660,768]{1,0:T(8,128)} reshape(f32[10,66,768]{2,1,0:T(8,128)S(1)} %maximum_convert_fusion) | data formatting | bytes 4055040 | tf_op jit(solution)/shard_map/convert_element_type | solution.py:37
  20.5 10.0 %fusion.7 = bf16[660,3072]{1,0:T(8,128)(2,1)} fusion(bf16[768,3072]{1,0:T(8,128)(2,1)} %param.20, f32[3072]{0:T(1024)S(1)} %copy-done.10, f32[660,768]{1,0:T(8,128)} %reshape.98, f32[768]{0:T(1024)S(1)} %copy-done.11, f32[768]{0:T(1024)S(1)} %copy-done.12), kind=kOutput, calls=%fused_computation.9 | convolution fusion | flops 3136066560 | bytes 10819584 | tf_op jit(solution)/shard_map/dot_general | solution.py:40
  30.5 4.8 %reshape.91 = bf16[10,66,3072]{2,1,0:T(8,128)(2,1)} reshape(bf16[660,3072]{1,0:T(8,128)(2,1)} %fusion.7) | data formatting | bytes 8110080 | tf_op jit(solution)/shard_map/reshape | solution.py:42
  35.3 2.8 %broadcast_select_fusion = bf16[10,66,3072]{2,1,0:T(8,128)(2,1)S(1)} fusion(bf16[10,66,3072]{2,1,0:T(8,128)(2,1)} %reshape.91, pred[10,66]{1,0:T(8,128)(4,1)S(1)} %broadcast_and_fusion), kind=kLoop, calls=%fused_computation.18 | loop fusion | flops 2027520 | bytes 8110740 | tf_op jit(solution)/shard_map/jit(_where)/select_n | solution.py:181
  38.1 8.9 %fusion.15 = bf16[8,64,3072]{2,1,0:T(8,128)(2,1)S(1)} fusion(bf16[10,66,3072]{2,1,0:T(8,128)(2,1)S(1)} %broadcast_select_fusion, f32[3072]{0:T(1024)S(1)} %copy-done.5, f32[3072]{0:T(1024)S(1)} %bitcast.42, f32[3072]{0:T(1024)S(1)} %bitcast.43, f32[3072]{0:T(1024)S(1)} %bitcast.36, f32[3072]{0:T(1024)S(1)} %bitcast.37, f32[3072]{0:T(1024)S(1)} %bitcast.38, ...), kind=kLoop, calls=%fused_computation.17 | loop fusion | flops 56623104 | bytes 31580160 | tf_op jit(solution)/shard_map/convert_element_type | solution.py:192
  47.1 2.6 %convolution_add_fusion = f32[512,768]{1,0:T(8,128)S(1)} fusion(bf16[512,3072]{1,0:T(8,128)(2,1)S(1)} %bitcast.30, bf16[3072,768]{1,0:T(8,128)(2,1)S(1)} %bitcast.45, f32[768]{0:T(1024)S(1)} %copy-done.13), kind=kOutput, calls=%fused_computation.32 | convolution fusion | flops 2416312320 | bytes 9440256 | tf_op jit(solution)/shard_map/dot_general | solution.py:194
  50.1 0.3 fusion.18
  50.4 0.4 fusion.21
  50.8 0.9 copy.20
  51.7 7.2 %all-to-all-start = ((bf16[32,2,1,1,8,768]{5,4,1,3,2,0:T(8,128)(2,1)}), bf16[32,2,1,1,8,768]{5,4,1,3,2,0:T(8,128)(2,1)S(1)}, u32[]{:S(2)}, u32[]{:S(2)}) async-start(bf16[32,2,1,1,8,768]{5,4,1,3,2,0:T(8,128)(2,1)} %bitcast.31), calls=%async_computation | async-start | bytes 1572864 | tf_op jit(solution)/shard_map/all_to_all | solution.py:217
  59.0 21.6 %all-to-all-done = bf16[32,2,1,1,8,768]{5,4,1,3,2,0:T(8,128)(2,1)S(1)} async-done(((bf16[32,2,1,1,8,768]{5,4,1,3,2,0:T(8,128)(2,1)}), bf16[32,2,1,1,8,768]{5,4,1,3,2,0:T(8,128)(2,1)S(1)}, u32[]{:S(2)}, u32[]{:S(2)}) %all-to-all-start) | async-done | bytes 786464 | tf_op jit(solution)/shard_map/all_to_all | solution.py:217
  80.6 2.0 %copy-done = bf16[768,2304]{1,0:T(8,128)(2,1)S(1)} copy-done((bf16[768,2304]{1,0:T(8,128)(2,1)S(1)}, bf16[768,2304]{1,0:T(8,128)(2,1)}, u32[]{:S(2)}) %copy-start) | copy-done | bytes 3538968
  82.6 8.0 %grid_attention.1 = bf16[512,768]{1,0:T(8,128)(2,1)S(1)} custom-call(bf16[512,768]{1,0:T(8,128)(2,1)S(1)} %bitcast.27, s32[512,1]{1,0:T(8,128)S(1)} %copy-done.2, s32[512,1]{1,0:T(8,128)S(1)} %copy-done.3, bf16[768,2304]{1,0:T(8,128)(2,1)S(1)} %copy-done, f32[1,2304]{1,0:T(1,128)S(1)} %broadcast_in_dim.40.qkv_bias_ref, bf16[768,768]{1,0:T(8,128)(2,1)S(1)} %copy-done.1, ...), custom_call_target="tpu_custom_call" | custom-call | flops 3019898880 | bytes 8388608 | tf_op jit(solution)/shard_map/grid_attention/pallas_call | solution.py:126
  90.7 24.0 %all_to_all.10 = bf16[32,2,1,1,8,768]{5,4,1,3,2,0:T(8,128)(2,1)S(1)} all-to-all(bf16[32,2,1,1,8,768]{5,4,1,3,2,0:T(8,128)(2,1)S(1)} %bitcast.28), channel_id=1, replica_groups=mesh['row'=4,'col'=8] {'row','col'}, dimensions={0} | all-to-all | bytes 1572864 | tf_op jit(solution)/shard_map/all_to_all | solution.py:234
  114.9 1.1 fusion.22
  (48 shorter events, 1.1 us)
Async XLA Ops:
  1.0 7.4 %collective-permute-start = (bf16[1,64,768]{2,1,0:T(8,128)(2,1)S(1)}, bf16[1,64,768]{2,1,0:T(8,128)(2,1)S(1)}, u32[]{:S(2)}, u32[]{:S(2)}) collective-permute-start(bf16[1,64,768]{2,1,0:T(8,128)(2,1)S(1)} %get-tuple-element.10), channel_id=1, source_target_pairs={{0,8},{8,16},{16,24},{1,9},{9,17},{17,25},{2,10},{10,18},{18,26},{... | collective-permute-start | bytes 294920 | tf_op jit(solution)/shard_map/ppermute | solution.py:27
  5.8 6.5 %collective-permute-start.1 = (bf16[1,64,768]{2,1,0:T(8,128)(2,1)S(1)}, bf16[1,64,768]{2,1,0:T(8,128)(2,1)S(1)}, u32[]{:S(2)}, u32[]{:S(2)}) collective-permute-start(bf16[1,64,768]{2,1,0:T(8,128)(2,1)S(1)} %get-tuple-element.9), channel_id=1, source_target_pairs={{8,0},{16,8},{24,16},{9,1},{17,9},{25,17},{10,2},{18,10},{26,18},{... | collective-permute-start | bytes 294920 | tf_op jit(solution)/shard_map/ppermute | solution.py:29
  8.3 12.1 %copy-start.10 = (f32[3072]{0:T(1024)S(1)}, f32[3072]{0:T(1024)}, u32[]{:S(2)}) copy-start(f32[3072]{0:T(1024)} %param.21) | copy-start | bytes 36868
  8.3 12.1 %copy-start.11 = (f32[768]{0:T(1024)S(1)}, f32[768]{0:T(1024)}, u32[]{:S(2)}) copy-start(f32[768]{0:T(1024)} %param.19) | copy-start | bytes 9220
  8.4 12.1 %copy-start.12 = (f32[768]{0:T(1024)S(1)}, f32[768]{0:T(1024)}, u32[]{:S(2)}) copy-start(f32[768]{0:T(1024)} %param.18) | copy-start | bytes 9220
  12.4 2.7 %collective-permute-start.2 = (bf16[10,1,768]{2,1,0:T(2,128)(2,1)S(1)}, bf16[10,1,768]{2,1,0:T(2,128)(2,1)S(1)}, u32[]{:S(2)}, u32[]{:S(2)}) collective-permute-start(bf16[10,1,768]{2,1,0:T(2,128)(2,1)S(1)} %get-tuple-element.7), channel_id=1, source_target_pairs={{0,1},{1,2},{2,3},{3,4},{4,5},{5,6},{6,7},{8,9},{9,10},{10,11},{11... | collective-permute-start | bytes 46088 | tf_op jit(solution)/shard_map/ppermute | solution.py:27
  13.7 4.9 %collective-permute-start.3 = (bf16[10,1,768]{2,1,0:T(2,128)(2,1)S(1)}, bf16[10,1,768]{2,1,0:T(2,128)(2,1)S(1)}, u32[]{:S(2)}, u32[]{:S(2)}) collective-permute-start(bf16[10,1,768]{2,1,0:T(2,128)(2,1)S(1)} %get-tuple-element.8), channel_id=1, source_target_pairs={{1,0},{2,1},{3,2},{4,3},{5,4},{6,5},{7,6},{9,8},{10,9},{11,10},{12... | collective-permute-start | bytes 46088 | tf_op jit(solution)/shard_map/ppermute | solution.py:29
  35.3 2.8 %copy-start.5 = (f32[3072]{0:T(1024)S(1)}, f32[3072]{0:T(1024)}, u32[]{:S(2)}) copy-start(f32[3072]{0:T(1024)} %param.23) | copy-start | bytes 36868
  35.3 11.8 %slice-start = ((s8[4718592]{0:T(1024)(128)(4,1)}), s8[4194304]{0:T(1024)(128)(4,1)S(1)}, s32[]{:S(2)}) async-start(s8[4718592]{0:T(1024)(128)(4,1)} %bitcast.44), calls=%async_computation.2 | async-start | bytes 8388608
  38.0 9.0 %slice-start.1 = ((s8[4718592]{0:T(1024)(128)(4,1)}), s8[524288]{0:T(1024)(128)(4,1)S(1)}, s32[]{:S(2)}) async-start(s8[4718592]{0:T(1024)(128)(4,1)} %bitcast.44), calls=%async_computation.3 | async-start | bytes 1048576
  38.1 9.0 %copy-start.13 = (f32[768]{0:T(1024)S(1)}, f32[768]{0:T(1024)}, u32[]{:S(2)}) copy-start(f32[768]{0:T(1024)} %param.25) | copy-start | bytes 9220
  47.1 2.7 %copy-start.4 = (bf16[8,64,768]{2,1,0:T(8,128)(2,1)S(1)}, bf16[8,64,768]{2,1,0:T(8,128)(2,1)}, u32[]{:S(2)}) copy-start(bf16[8,64,768]{2,1,0:T(8,128)(2,1)} %param.17) | copy-start | bytes 2359300
  47.1 3.3 %copy-start.7 = (f32[768]{0:T(1024)S(1)}, f32[768]{0:T(1024)}, u32[]{:S(2)}) copy-start(f32[768]{0:T(1024)} %param.27) | copy-start | bytes 9220
  47.1 3.3 %copy-start.8 = (f32[768]{0:T(1024)S(1)}, f32[768]{0:T(1024)}, u32[]{:S(2)}) copy-start(f32[768]{0:T(1024)} %param.26) | copy-start | bytes 9220
  49.7 9.2 %copy-start.6 = (f32[2304]{0:T(1024)S(1)}, f32[2304]{0:T(1024)}, u32[]{:S(2)}) copy-start(f32[2304]{0:T(1024)} %param.29) | copy-start | bytes 27652
  49.7 9.2 %copy-start.9 = (f32[768]{0:T(1024)S(1)}, f32[768]{0:T(1024)}, u32[]{:S(2)}) copy-start(f32[768]{0:T(1024)} %param.31) | copy-start | bytes 9220
  49.7 30.9 %copy-start.1 = (bf16[768,768]{1,0:T(8,128)(2,1)S(1)}, bf16[768,768]{1,0:T(8,128)(2,1)}, u32[]{:S(2)}) copy-start(bf16[768,768]{1,0:T(8,128)(2,1)} %out_weight_ref.1) | copy-start | bytes 3538948
  49.8 30.9 %copy-start.2 = (s32[512,1]{1,0:T(8,128)S(1)}, s32[512,1]{1,0:T(8,128)}, u32[]{:S(2)}) copy-start(s32[512,1]{1,0:T(8,128)} %constant.48.pick_ref) | copy-start | bytes 6148
  49.8 30.8 %copy-start.3 = (s32[512,1]{1,0:T(8,128)S(1)}, s32[512,1]{1,0:T(8,128)}, u32[]{:S(2)}) copy-start(s32[512,1]{1,0:T(8,128)} %constant.49.place_ref) | copy-start | bytes 6148
  51.7 28.9 %all-to-all-start = ((bf16[32,2,1,1,8,768]{5,4,1,3,2,0:T(8,128)(2,1)}), bf16[32,2,1,1,8,768]{5,4,1,3,2,0:T(8,128)(2,1)S(1)}, u32[]{:S(2)}, u32[]{:S(2)}) async-start(bf16[32,2,1,1,8,768]{5,4,1,3,2,0:T(8,128)(2,1)} %bitcast.31), calls=%async_computation | async-start | bytes 1572864 | tf_op jit(solution)/shard_map/all_to_all | solution.py:217
  80.6 2.0 %copy-start = (bf16[768,2304]{1,0:T(8,128)(2,1)S(1)}, bf16[768,2304]{1,0:T(8,128)(2,1)}, u32[]{:S(2)}) copy-start(bf16[768,2304]{1,0:T(8,128)(2,1)} %qkv_weight_ref.1) | copy-start | bytes 10616836

commit v2 on v1

v2 whole, which is shorter than its diff:
```python
import functools
import math

import jax
import jax.numpy as jnp
import numpy as np
from jax import lax
from jax.experimental import pallas as pl
from jax.experimental.pallas import tpu as pltpu
from jax.sharding import PartitionSpec as P

HEADS = 24
HEAD_DIM = 32
GRID = 8
LANES = 128
PACK = LANES // HEAD_DIM


def gelu(v):
    half = 0.5 * v
    inner = v * (0.7978845608028654 + 0.035677408136300125 * (v * v))
    return half + half * jnp.tanh(inner)


def in_hbm(array):
    return pltpu.with_memory_space_constraint(array, pltpu.HBM)


def row_of(ref, cols=slice(None)):
    return ref[cols].reshape(1, -1)


def fetch(source, target, sems, start, count):
    block = target.shape[-1]
    return [
        pltpu.make_async_copy(
            source.at[:, pl.ds((start + i) * block, block)], target.at[i], sems.at[i]
        )
        for i in range(count)
    ]


FOLD = 8


def one_hot(index_ref, count):
    column = lax.broadcasted_iota(jnp.int32, (index_ref.shape[0], count), 1)
    return (column == index_ref[...]).astype(jnp.float32).astype(jnp.bfloat16)


def shuffled(index_ref, values):
    pick = one_hot(index_ref, values.shape[0])
    return jnp.dot(pick, values, preferred_element_type=jnp.float32).astype(jnp.bfloat16)


def whole(array):
    return pl.BlockSpec(array.shape, lambda i: (0,) * array.ndim)


OUTSIDE = pl.BlockSpec(memory_space=pltpu.HBM)


INSIDE = pl.BlockSpec(memory_space=pltpu.VMEM)
BLOCK = 256
TALL = 128


def like(*arrays):
    return [jax.ShapeDtypeStruct(array.shape, array.dtype) for array in arrays]


def expand_all(start, normed_ref, bias_ref, copies, held_ref, o_ref):
    steps, _, block = held_ref.shape
    count = normed_ref.shape[0]
    for i in range(steps):
        copies[i].wait()
        cols = slice(i * block, (i + 1) * block)
        bias = row_of(bias_ref, slice((start + i) * block, (start + i + 1) * block))
        for lo in range(0, count, TALL):
            rows = slice(lo, lo + TALL)
            part = jnp.dot(normed_ref[rows], held_ref[i], preferred_element_type=jnp.float32)
            o_ref[rows, cols] = gelu(part + bias)


def normalize(x, scale_ref, shift_ref):
    return (x.astype(jnp.float32) * row_of(scale_ref) + row_of(shift_ref)).astype(jnp.bfloat16)


def expand_low_kernel(
    x_ref,
    fold_ref,
    columns_ref,
    scale_ref,
    shift_ref,
    bias_ref,
    weight_ref,
    o_ref,
    folded_ref,
    edges_ref,
    held_ref,
    normed_ref,
    sems,
):
    copies = fetch(weight_ref, held_ref, sems, 0, held_ref.shape[0])
    for copy in copies:
        copy.start()
    x = x_ref[...]
    folded = shuffled(fold_ref, x)
    folded_ref[...] = folded
    edges_ref[...] = shuffled(columns_ref, x)
    normed_ref[...] = normalize(folded, scale_ref, shift_ref)
    expand_all(0, normed_ref, bias_ref, copies, held_ref, o_ref)


def expand_high_kernel(
    scale_ref,
    shift_ref,
    bias_ref,
    folded_ref,
    _,
    weight_ref,
    project_ref,
    o_ref,
    held_ref,
    project_held_ref,
    normed_ref,
    sems,
    project_sem,
):
    steps = held_ref.shape[0]
    copies = fetch(weight_ref, held_ref, sems, steps, steps)
    project = pltpu.make_async_copy(project_ref, project_held_ref, project_sem)
    for copy in copies:
        copy.start()
    project.start()
    normed_ref[...] = normalize(folded_ref[...], scale_ref, shift_ref)
    expand_all(steps, normed_ref, bias_ref, copies, held_ref, o_ref)
    project.wait()


def expand_low(fold, columns, tokens, scale, shift, weight, bias):
    count, channels = tokens.shape
    width = weight.shape[1] // 2
    steps = width // BLOCK
    smalls = [tokens, fold, columns, scale, shift, bias]
    return pl.pallas_call(
        expand_low_kernel,
        grid=(1,),
        out_shape=[
            jax.ShapeDtypeStruct((count, width), jnp.float32),
            jax.ShapeDtypeStruct((count, channels), jnp.bfloat16),
            jax.ShapeDtypeStruct((columns.shape[0], channels), jnp.bfloat16),
            jax.ShapeDtypeStruct((steps, channels, BLOCK), jnp.bfloat16),
        ],
        in_specs=[whole(array) for array in smalls] + [OUTSIDE],
        out_specs=[INSIDE] * 4,
        scratch_shapes=[
            pltpu.VMEM((count, channels), jnp.bfloat16),
            pltpu.SemaphoreType.DMA((steps,)),
        ],
        cost_estimate=pl.CostEstimate(
            flops=2 * count * channels * width,
            bytes_accessed=2 * channels * width,
            transcendentals=count * width,
        ),
        compiler_params=pltpu.CompilerParams(vmem_limit_bytes=12 << 20),
        name="expand_low",
    )(*[in_hbm(array) for array in smalls], in_hbm(weight))


def expand_high(folded, after, scale, shift, weight, bias, project_weight):
    count, channels = folded.shape
    width = weight.shape[1] // 2
    steps = width // BLOCK
    smalls = [scale, shift, bias]
    return pl.pallas_call(
        expand_high_kernel,
        grid=(1,),
        out_shape=[
            jax.ShapeDtypeStruct((count, width), jnp.float32),
            jax.ShapeDtypeStruct((steps, channels, BLOCK), jnp.bfloat16),
            *like(project_weight),
        ],
        in_specs=[whole(array) for array in smalls]
        + [INSIDE, pl.BlockSpec(memory_space=pl.ANY), OUTSIDE, OUTSIDE],
        out_specs=[INSIDE] * 3,
        scratch_shapes=[
            pltpu.VMEM((count, channels), jnp.bfloat16),
            pltpu.SemaphoreType.DMA((steps,)),
            pltpu.SemaphoreType.DMA,
        ],
        cost_estimate=pl.CostEstimate(
            flops=2 * count * channels * width,
            bytes_accessed=6 * channels * width,
            transcendentals=count * width,
        ),
        compiler_params=pltpu.CompilerParams(vmem_limit_bytes=12 << 20),
        name="expand_high",
    )(*[in_hbm(array) for array in smalls], folded, after, in_hbm(weight), in_hbm(project_weight))


def edges_kernel(tall, first_row_ref, second_row_ref, edges_ref, first_ref, second_ref):
    f32 = jnp.float32
    row_even = lax.rem(lax.axis_index("row"), 2) == 0
    col_even = lax.rem(lax.axis_index("col"), 2) == 0
    strip = first_ref.shape[0]
    last = first_row_ref.shape[0]
    spot = lax.broadcasted_iota(jnp.int32, (strip, 1), 0)

    def column(side, at):
        first = first_row_ref[at : at + 1].astype(f32)
        second = second_row_ref[at : at + 1].astype(f32)
        top = jnp.where(row_even, second, first)
        bottom = jnp.where(row_even, first, second)
        middle = edges_ref[side * strip : (side + 1) * strip].astype(f32)
        return jnp.where(spot == 0, top, jnp.where(spot == tall - 1, bottom, middle))

    left, right = column(0, 0), column(1, last - 1)
    first_ref[...] = jnp.where(col_even, right, left).astype(jnp.bfloat16)
    second_ref[...] = jnp.where(col_even, left, right).astype(jnp.bfloat16)


def edges_to_send(tall, first_row, second_row, edges):
    shape = jax.ShapeDtypeStruct((edges.shape[0] // 2, edges.shape[1]), edges.dtype)
    return pl.pallas_call(
        functools.partial(edges_kernel, tall),
        out_shape=[shape, shape],
        in_specs=[INSIDE] * 3,
        out_specs=[INSIDE] * 2,
        compiler_params=pltpu.CompilerParams(vmem_limit_bytes=2 << 20),
        name="edges",
    )(first_row, second_row, edges)


def conv_kernel(
    shape,
    halo_order_ref,
    natural_ref,
    order_ref,
    scale_ref,
    shift_ref,
    expand_bias_ref,
    depth_kernel_ref,
    depth_bias_ref,
    project_bias_ref,
    gain_ref,
    offset_ref,
    low_ref,
    high_ref,
    first_row_ref,
    second_row_ref,
    first_col_ref,
    second_col_ref,
    low_weight_ref,
    high_weight_ref,
    project_weight_ref,
    features_ref,
    qkv_weight_ref,
    out_weight_ref,
    after_ref,
    attn_ref,
    qkv_held_ref,
    out_held_ref,
    normed_ref,
    halo_hidden_ref,
    left_ref,
    right_ref,
    depth_ref,
    sems,
):
    f32, bf16 = jnp.float32, jnp.bfloat16
    rows, cols = shape
    planes = cols // FOLD
    tall = rows + 2
    strip = first_col_ref.shape[0]
    prefetch = [
        pltpu.make_async_copy(qkv_weight_ref, qkv_held_ref, sems.at[0]),
        pltpu.make_async_copy(out_weight_ref, out_held_ref, sems.at[1]),
    ]
    for copy in prefetch:
        copy.start()

    row_at, col_at = lax.axis_index("row"), lax.axis_index("col")
    row_even, col_even = lax.rem(row_at, 2) == 0, lax.rem(col_at, 2) == 0
    has_top = (row_at > 0).astype(f32)
    has_bottom = (row_at < lax.axis_size("row") - 1).astype(f32)
    has_left = (col_at > 0).astype(f32)
    has_right = (col_at < lax.axis_size("col") - 1).astype(f32)
    top_at = jnp.where(row_even, cols, 0)
    bottom_at = jnp.where(row_even, 0, cols)
    left_at = 2 * cols + jnp.where(col_even, strip, 0)
    right_at = 2 * cols + jnp.where(col_even, 0, strip)
    spot = lax.broadcasted_iota(jnp.int32, (2 * cols + 2 * strip, 1), 0)
    first_there = jnp.where(row_even, has_bottom, has_top)
    second_there = jnp.where(row_even, has_top, has_bottom)
    near_there = jnp.where(col_even, has_right, has_left)
    far_there = jnp.where(col_even, has_left, has_right)
    place = lax.rem(spot, strip)
    ends = jnp.where(place == 0, has_top, jnp.where(place == tall - 1, has_bottom, 1.0))
    keep = jnp.where(
        spot < cols,
        first_there,
        jnp.where(
            spot < 2 * cols,
            second_there,
            ends * jnp.where(spot < 2 * cols + strip, near_there, far_there),
        ),
    )

    halo = jnp.concatenate(
        [first_row_ref[...], second_row_ref[...], first_col_ref[...], second_col_ref[...]], axis=0
    )
    normed_ref[...] = shuffled(halo_order_ref, normalize(halo, scale_ref, shift_ref))

    def convolve(step, hidden_ref, weight_ref, offset):
        base = pl.multiple_of((step + offset) * BLOCK, BLOCK)
        part = jnp.dot(normed_ref[...], weight_ref[step], preferred_element_type=f32)
        bias = expand_bias_ref[pl.ds(base, BLOCK)].reshape(1, BLOCK)
        halo_hidden_ref[...] = gelu(part + bias) * keep
        for lane in range(BLOCK // LANES):
            lanes = slice(lane * LANES, (lane + 1) * LANES)
            inner = pl.ds(pl.multiple_of(step * BLOCK + lane * LANES, LANES), LANES)
            outer = pl.ds(pl.multiple_of(base + lane * LANES, LANES), LANES)
            left = halo_hidden_ref[pl.ds(pl.multiple_of(left_at, 8), strip), lanes]
            right = halo_hidden_ref[pl.ds(pl.multiple_of(right_at, 8), strip), lanes]

            def cell(r, j):
                if r == 0 or r == tall - 1:
                    at = (top_at if r == 0 else bottom_at) + j * FOLD
                    return halo_hidden_ref[pl.ds(pl.multiple_of(at, 8), FOLD), lanes]
                at = ((r - 1) * planes + j) * FOLD
                return hidden_ref[at : at + FOLD, inner]

            for r in range(tall):
                left_ref[lane, r, 8 : 8 + FOLD, :] = cell(r, planes - 1)
                left_ref[lane, r, 7:8, :] = left[r : r + 1]
                right_ref[lane, r, 0:FOLD, :] = cell(r, 0)
                right_ref[lane, r, FOLD : FOLD + 1, :] = right[r : r + 1]

            def shifted(r, j):
                if j < 0:
                    return left_ref[lane, r, 7 : 7 + FOLD, :]
                if j == planes:
                    return right_ref[lane, r, 1 : 1 + FOLD, :]
                return cell(r, j)

            taps = [
                [
                    jnp.broadcast_to(depth_kernel_ref[a, b : b + 1, outer], (FOLD, LANES))
                    for b in range(3)
                ]
                for a in range(3)
            ]
            bias = jnp.broadcast_to(depth_bias_ref[outer].reshape(1, LANES), (FOLD, LANES))
            pair = 2
            for start in range(0, planes, pair):
                sums = [[None] * rows for _ in range(pair)]
                for r in range(tall):
                    near = [shifted(r, start - 1 + b) for b in range(pair + 2)]
                    for k in range(pair):
                        for a in range(3):
                            h = r - a
                            if 0 <= h < rows:
                                line = near[k] * taps[a][0] + near[k + 1] * taps[a][1]
                                line = line + near[k + 2] * taps[a][2]
                                old = sums[k][h]
                                sums[k][h] = line + (bias if old is None else old)
                    h = r - 2
                    if h >= 0:
                        lo = (h * planes + start) * FOLD
                        depth_ref[lo : lo + pair * FOLD, outer] = jnp.concatenate(
                            [gelu(sums[k][h]) for k in range(pair)], axis=0
                        ).astype(bf16)

    half = low_weight_ref.shape[0]

    def low_step(step, carry):
        convolve(step, low_ref, low_weight_ref, 0)
        return carry

    def high_step(step, carry):
        convolve(step, high_ref, high_weight_ref, half)
        return carry

    lax.fori_loop(0, half, low_step, 0)
    lax.fori_loop(0, half, high_step, 0)

    group = 256
    normals, afters = [], []
    for lo in range(0, rows * cols, group):
        part = slice(lo, lo + group)
        total = jnp.dot(depth_ref[part], project_weight_ref[...], preferred_element_type=f32)
        after = features_ref[part].astype(f32) + total + row_of(project_bias_ref)
        after = after.astype(bf16)
        wide = after.astype(f32)
        center = wide - jnp.mean(wide, axis=-1, keepdims=True)
        spread = jnp.mean(center * center, axis=-1, keepdims=True)
        normal = center * lax.rsqrt(spread + 1e-06) * row_of(gain_ref) + row_of(offset_ref)
        afters.append(after)
        normals.append(normal.astype(bf16))
    after_ref[...] = shuffled(natural_ref, jnp.concatenate(afters, axis=0))
    attn_ref[...] = shuffled(order_ref, jnp.concatenate(normals, axis=0))
    for copy in prefetch:
        copy.wait()


def convolve(shape, smalls, larges, qkv_weight, out_weight):
    rows, cols = shape
    features = larges[-1]
    count, channels = features.shape
    width = larges[0].shape[1] * 2
    around = smalls[0].shape[0]
    return pl.pallas_call(
        functools.partial(conv_kernel, shape),
        grid=(1,),
        out_shape=like(features, features, qkv_weight, out_weight),
        in_specs=[whole(array) for array in smalls] + [INSIDE] * len(larges) + [OUTSIDE] * 2,
        out_specs=[INSIDE] * 4,
        scratch_shapes=[
            pltpu.VMEM((around, channels), jnp.bfloat16),
            pltpu.VMEM((around, BLOCK), jnp.float32),
            pltpu.VMEM((BLOCK // LANES, rows + 2, FOLD + 8, LANES), jnp.float32),
            pltpu.VMEM((BLOCK // LANES, rows + 2, FOLD + 8, LANES), jnp.float32),
            pltpu.VMEM((count, width), jnp.bfloat16),
            pltpu.SemaphoreType.DMA((2,)),
        ],
        cost_estimate=pl.CostEstimate(
            flops=4 * count * channels * width,
            bytes_accessed=4 * channels * width,
            transcendentals=count * width,
        ),
        compiler_params=pltpu.CompilerParams(vmem_limit_bytes=24 << 20),
        name="depthwise_project",
    )(*[in_hbm(array) for array in smalls], *larges, in_hbm(qkv_weight), in_hbm(out_weight))


def swap(cells, axis, count, odd_pairs):
    pairs = [(i, i + 1) for i in range(1 if odd_pairs else 0, count - 1, 2)]
    return lax.ppermute(cells, axis, pairs + [(j, i) for i, j in pairs])


def attend_kernel(
    group_size,
    x_ref,
    pick_ref,
    place_ref,
    qkv_weight_ref,
    qkv_bias_ref,
    out_weight_ref,
    out_bias_ref,
    o_ref,
    qkv_ref,
    mixed_ref,
    probs_ref,
):
    count, channels = x_ref.shape
    f32, bf16 = jnp.float32, jnp.bfloat16
    x = shuffled(pick_ref, x_ref[...])
    step = 256
    for lo in range(0, 3 * channels, step):
        cols = slice(lo, lo + step)
        part = jnp.dot(x, qkv_weight_ref[:, cols], preferred_element_type=f32)
        qkv_ref[:, cols] = (part + row_of(qkv_bias_ref, cols)).astype(bf16)

    wide = PACK * group_size
    lane = lax.broadcasted_iota(jnp.int32, (wide, LANES), 1) // HEAD_DIM
    row = lax.broadcasted_iota(jnp.int32, (wide, LANES), 0) // group_size
    own = (lane == row).astype(f32).astype(bf16)
    block_row = lax.broadcasted_iota(jnp.int32, (wide, wide), 0) // group_size
    block_col = lax.broadcasted_iota(jnp.int32, (wide, wide), 1) // group_size
    same = (block_row == block_col).astype(f32).astype(bf16)
    scale = math.log2(math.e) / math.sqrt(HEAD_DIM)
    top = float(jnp.finfo(bf16).max)
    chunks = channels // LANES

    def one_group(group, carry):
        rows = pl.ds(pl.multiple_of(group * group_size, group_size), group_size)
        for chunk in range(chunks):
            lo = chunk * LANES
            query = qkv_ref[rows, lo : lo + LANES]
            key = qkv_ref[rows, channels + lo : channels + lo + LANES]
            keys = jnp.concatenate([key] * PACK, axis=0) * own
            scores = lax.dot_general(
                query, keys, (((1,), (1,)), ((), ())), preferred_element_type=f32
            )
            probs_ref[chunk * group_size : (chunk + 1) * group_size, :] = jnp.exp2(scores * scale)
        weights = probs_ref[...]
        total = jnp.dot(jnp.minimum(weights, top).astype(bf16), same, preferred_element_type=f32)
        probs = (weights / total).astype(bf16)
        for chunk in range(chunks):
            lo = chunk * LANES
            value = qkv_ref[rows, 2 * channels + lo : 2 * channels + lo + LANES]
            values = jnp.concatenate([value] * PACK, axis=0) * own
            mixed_ref[rows, lo : lo + LANES] = jnp.dot(
                probs[chunk * group_size : (chunk + 1) * group_size],
                values,
                preferred_element_type=f32,
            ).astype(bf16)
        return carry

    lax.fori_loop(0, count // group_size, one_group, 0)
    result = jnp.dot(mixed_ref[...], out_weight_ref[...], preferred_element_type=f32)
    o_ref[...] = shuffled(place_ref, (result + row_of(out_bias_ref)).astype(bf16))


def attend(tokens, order, group_size, qkv_weight, qkv_bias, out_weight, out_bias):
    count, channels = tokens.shape
    pick = np.asarray(order, np.int32)
    place = np.argsort(pick).astype(np.int32)
    inside = pl.BlockSpec(memory_space=pltpu.VMEM)
    smalls = [jnp.asarray(pick)[:, None], jnp.asarray(place)[:, None], qkv_bias, out_bias]
    pick, place, qkv_bias, out_bias = [in_hbm(array) for array in smalls]
    arrays = [tokens, pick, place, qkv_weight, qkv_bias, out_weight, out_bias]
    specs = [whole(array) for array in arrays]
    specs[0] = specs[3] = specs[5] = inside
    return pl.pallas_call(
        functools.partial(attend_kernel, group_size),
        grid=(1,),
        out_shape=jax.ShapeDtypeStruct((count, channels), jnp.bfloat16),
        in_specs=specs,
        out_specs=inside,
        scratch_shapes=[
            pltpu.VMEM((count, 3 * channels), jnp.bfloat16),
            pltpu.VMEM((count, channels), jnp.bfloat16),
            pltpu.VMEM((channels // LANES * group_size, PACK * group_size), jnp.float32),
        ],
        cost_estimate=pl.CostEstimate(
            flops=10 * count * channels * channels, bytes_accessed=8 << 20, transcendentals=1 << 20
        ),
        compiler_params=pltpu.CompilerParams(vmem_limit_bytes=16 << 20),
        name="grid_attention",
    )(*arrays)


def per_device(
    features,
    norm_scale,
    norm_shift,
    expand_weight,
    expand_bias,
    depth_kernel,
    depth_bias,
    project_weight,
    project_bias,
    attn_gain,
    attn_shift,
    qkv_weight,
    qkv_bias,
    out_weight,
    out_bias,
):
    tile_rows, tile_cols, channels = features.shape
    row_count = lax.axis_size("row")
    col_count = lax.axis_size("col")
    row_at = lax.axis_index("row")
    flat = features.reshape(-1, channels)
    tall = tile_rows + 2
    strip = -(-tall // 16) * 16
    planes = tile_cols // FOLD
    one_row = np.arange(tile_cols).reshape(FOLD, planes).T.reshape(-1)
    fold = (np.arange(tile_rows)[:, None] * tile_cols + one_row[None]).reshape(-1)
    unfold = np.argsort(fold)
    columns = np.full((2, strip), -1)
    columns[0, 1 : tall - 1] = np.arange(tile_rows) * tile_cols
    columns[1, 1 : tall - 1] = np.arange(tile_rows) * tile_cols + tile_cols - 1

    def index_array(values):
        return jnp.asarray(np.asarray(values, np.int32).reshape(-1))[:, None]

    row_even = row_at % 2 == 0
    near = lax.dynamic_slice_in_dim(features, jnp.where(row_even, tile_rows - 1, 0), 1, 0)[0]
    far = lax.dynamic_slice_in_dim(features, jnp.where(row_even, 0, tile_rows - 1), 1, 0)[0]
    first_row = swap(near, "row", row_count, False)
    second_row = swap(far, "row", row_count, True)
    low, folded, edges, low_weight = expand_low(
        index_array(fold),
        index_array(columns),
        flat,
        norm_scale,
        norm_shift,
        expand_weight,
        expand_bias,
    )
    first_col, second_col = edges_to_send(tall, first_row, second_row, edges)
    high, high_weight, project_held = expand_high(
        folded, first_col, norm_scale, norm_shift, expand_weight, expand_bias, project_weight
    )
    first_col = swap(first_col, "col", col_count, False)
    second_col = swap(second_col, "col", col_count, True)
    fold_row = max(1, GRID // row_count)
    fold_col = max(1, GRID // col_count)
    parity_row = max(1, row_count // GRID)
    parity_col = max(1, col_count // GRID)
    block_row = tile_rows // (fold_row * row_count)
    block_col = tile_cols // (fold_col * col_count)
    source = np.arange(tile_rows * tile_cols).reshape(
        fold_row, row_count, block_row, fold_col, col_count, block_col
    )
    source = source.transpose(1, 4, 0, 2, 3, 5).reshape(-1)
    around = np.concatenate(
        [one_row, tile_cols + one_row, 2 * tile_cols + np.arange(2 * strip)]
    )
    after_conv, ordered, qkv_weight, out_weight = convolve(
        (tile_rows, tile_cols),
        [
            index_array(around),
            index_array(unfold),
            index_array(unfold[source]),
            norm_scale,
            norm_shift,
            expand_bias,
            depth_kernel,
            depth_bias,
            project_bias,
            attn_gain,
            attn_shift,
        ],
        [
            low,
            high,
            first_row,
            second_row,
            first_col,
            second_col,
            low_weight,
            high_weight,
            project_held,
            folded,
        ],
        qkv_weight,
        out_weight,
    )
    after_conv = after_conv.reshape(features.shape)
    ordered = ordered.reshape(
        row_count * col_count, fold_row, block_row, fold_col, block_col, channels
    )
    received = lax.all_to_all(ordered, ("row", "col"), split_axis=0, concat_axis=0, tiled=True)
    tokens = received.reshape(-1, channels)
    layout = np.arange(tokens.shape[0]).reshape(
        row_count // parity_row,
        parity_row,
        col_count // parity_col,
        parity_col,
        fold_row,
        block_row,
        fold_col,
        block_col,
    )
    order = layout.transpose(1, 3, 5, 7, 0, 2, 4, 6)
    group_size = math.prod(order.shape[4:])
    answered = attend(
        tokens, order.reshape(-1), group_size, qkv_weight, qkv_bias, out_weight, out_bias
    ).reshape(received.shape)
    returned = lax.all_to_all(answered, ("row", "col"), split_axis=0, concat_axis=0, tiled=True)
    returned_tiles = returned.reshape(
        row_count, col_count, fold_row, block_row, fold_col, block_col, channels
    ).transpose(2, 0, 3, 4, 1, 5, 6)
    attended = returned_tiles.reshape(tile_rows, tile_cols, channels)
    return (after_conv.astype(jnp.float32) + attended.astype(jnp.float32)).astype(jnp.bfloat16)


def solution(mesh):
    return jax.shard_map(
        per_device,
        mesh=mesh,
        in_specs=(P("row", "col", None),) + (P(),) * 14,
        out_specs=P("row", "col", None),
        check_vma=False,
    )
```

time: 117 us -> 95.4 us (0.82)
  waiting for transfers between devices: 27.9 us -> 0.01 us
  blocking collectives: 24 us -> 49.5 us
  Pallas kernels: 8.03 us -> 32.9 us
  other arithmetic: 14.3 us -> 1.28 us
  matrix products: 12.6 us -> 0 us
  local copies, waits for them, and re-layouts: 12.8 us -> 1.08 us
  starting transfers between devices: 15.9 us -> 10.1 us
    all_to_all x0 -> x1, blocking collectives: none -> 25.6 us  [per_device(): lax.all_to_all(ordered, ('row', 'col'), split_axis=0, concat_axis=0, tile...]
    pallas_call x1 -> x5, Pallas kernels: 8.03 us -> 32.9 us  [the longest x1 14.5 us: convolve(): pl.pallas_call(functools.partial(conv_kernel, shape), grid=(1,), out_shap...]
    all_to_all x1 -> x0, waiting for transfers between devices: 21.6 us -> none  [per_device(): lax.all_to_all(ordered, ('row', 'col'), split_axis=0, concat_axis=0, tile...]
    dot_general x2 -> x0, matrix products: 12.6 us -> none  [the longest x1 10 us: expand_cells(): jnp.dot(flat_rows, expand_weight, preferred_element_type=jnp.float32)]
    convert_element_type x3 -> x0, other arithmetic: 9.57 us -> none  [the longest x1 8.95 us: per_device(): depthwise = jax.nn.gelu(summed + depth_bias).astype(jnp.bfloat16)]
    all_to_all x1 -> x0, starting transfers between devices: 7.18 us -> none  [per_device(): lax.all_to_all(ordered, ('row', 'col'), split_axis=0, concat_axis=0, tile...]
    ppermute x4, waiting for transfers between devices: 6.31 us -> 0.01 us  [swap(): return lax.ppermute(cells, axis, pairs + [(j, i) for i, j in pairs])]
    reshape x2 -> x0, local copies, waits for them, and re-layouts: 5.7 us -> none  [the longest x1 4.76 us: expand_cells(): hidden.astype(jnp.bfloat16)]
  transfers between devices with their start and end apart: 5 -> 4, of which waited for: 3 -> 0; matrix products, arithmetic and copies ran while one was open for 2% -> 0% of each run, Pallas kernels for 0% -> 10%
where the time goes in v2:
time: 95.4 us; the launch traced here: 95 us
  blocking collectives  49.5 us (52%)
  Pallas kernels  32.9 us (34%)
  starting transfers between devices  10.1 us (11%)
  other arithmetic  1.28 us (1%)
  local copies, waits for them, and re-layouts  1.08 us (1%)
    all_to_all x1, blocking collectives, per_device(): lax.all_to_all(ordered, ('row', 'col'), split_axis=0, concat_axis=0, tile...  25.6 us
    all_to_all x1, blocking collectives, per_device(): lax.all_to_all(answered, ('row', 'col'), split_axis=0, concat_axis=0, til...  24 us
    pallas_call x1, Pallas kernels, convolve(): pl.pallas_call(functools.partial(conv_kernel, shape), grid=(1,), out_shap...  14.5 us
    ppermute x4, starting transfers between devices, swap(): return lax.ppermute(cells, axis, pairs + [(j, i) for i, j in pairs])  10.1 us
    pallas_call x1, Pallas kernels, attend(): pl.pallas_call(functools.partial(attend_kernel, group_size), grid=(1,), o...  9.06 us
    pallas_call x1, Pallas kernels, expand_low(): pl.pallas_call(expand_low_kernel, grid=(1,), out_shape=[jax.ShapeDtypeStr...  4.88 us
    pallas_call x1, Pallas kernels, expand_high(): pl.pallas_call(expand_high_kernel, grid=(1,), out_shape=[jax.ShapeDtypeSt...  4.44 us
  transfers between devices with their start and end apart: 4, of which 0 were waited for; matrix products, arithmetic and copies ran while one was open for 0% of the time, Pallas kernels for 10%

profile of v2, /device:TPU:0, one launch (start us, length us, event | category | flops | bytes accessed | tf_op | source)
XLA Modules:
  0.0 95.0 jit_solution(6950858214247464893)
XLA Ops:
  0.0 1.0 %dynamic-slice_bitcast_fusion = (bf16[64,768]{1,0:T(8,128)(2,1)S(1)}, bf16[64,768]{1,0:T(8,128)(2,1)S(1)}) fusion(bf16[8,64,768]{2,1,0:T(8,128)(2,1)} %param.22, s32[]{:T(128)S(6)} %select_n.18, s32[]{:T(128)S(6)} %select_n.17), kind=kLoop, calls=%fused_computation.3 | loop fusion | bytes 393224 | tf_op jit(solution)/shard_map/squeeze | solution.py:572
  1.0 0.7 collective-permute-start.1
  1.6 5.8 %collective-permute-start = (bf16[64,768]{1,0:T(8,128)(2,1)S(1)}, bf16[64,768]{1,0:T(8,128)(2,1)S(1)}, u32[]{:S(2)}, u32[]{:S(2)}) collective-permute-start(bf16[64,768]{1,0:T(8,128)(2,1)S(1)} %get-tuple-element.32), channel_id=1, source_target_pairs={{0,8},{16,24},{8,0},{24,16},{1,9},{17,25},{9,1},{25,17},{2,10},{18... | collective-permute-start | bytes 294920 | tf_op jit(solution)/shard_map/ppermute | solution.py:439
  7.4 4.9 %expand_low.1 = (f32[512,1536]{1,0:T(8,128)S(1)}, bf16[512,768]{1,0:T(8,128)(2,1)S(1)}, bf16[32,768]{1,0:T(8,128)(2,1)S(1)}, bf16[6,768,256]{2,1,0:T(8,128)(2,1)S(1)}) custom-call(bf16[512,768]{1,0:T(8,128)(2,1)} %bitcast.25, s32[512,1]{1,0:T(8,128)} %constant.43.fold_ref.natural_ref, s32[32,1]{1,0:T(8,128)} %constant.45.columns_ref, f32[768]{0:T(1024)} %scale_ref.5, ...), custom_call_target="tpu_custom_call" | custom-call | flops 1207959552 | bytes 2359296 | tf_op jit(solution)/shard_map/expand_low/pallas_call | solution.py:146
  12.3 0.0 collective-permute-done.1.second_row_ref
  12.3 0.0 collective-permute-done.first_row_ref
  12.4 0.7 collective-permute-start.3
  13.0 3.0 %collective-permute-start.2 = (bf16[16,768]{1,0:T(8,128)(2,1)S(1)}, bf16[16,768]{1,0:T(8,128)(2,1)S(1)}, u32[]{:S(2)}, u32[]{:S(2)}) collective-permute-start(bf16[16,768]{1,0:T(8,128)(2,1)S(1)} %get-tuple-element.21._), channel_id=1, source_target_pairs={{0,1},{2,3},{4,5},{6,7},{1,0},{3,2},{5,4},{7,6},{8,9},{10,11},{12,... | collective-permute-start | bytes 73736 | tf_op jit(solution)/shard_map/ppermute | solution.py:439
  16.0 4.4 %expand_high.1 = (f32[512,1536]{1,0:T(8,128)S(1)}, bf16[6,768,256]{2,1,0:T(8,128)(2,1)S(1)}, bf16[3072,768]{1,0:T(8,128)(2,1)S(1)}) custom-call(f32[768]{0:T(1024)} %scale_ref.5, f32[768]{0:T(1024)} %shift_ref.5, f32[3072]{0:T(1024)} %expand_bias_ref.1, bf16[512,768]{1,0:T(8,128)(2,1)S(1)} %get-tuple-element.19.folded_ref.features_ref, ...), custom_call_target="tpu_custom_call" | custom-call | flops 1207959552 | bytes 7077888 | tf_op jit(solution)/shard_map/expand_high/pallas_call | solution.py:176
  20.5 0.0 collective-permute-done.3.second_col_ref
  20.5 0.0 collective-permute-done.2.first_col_ref
  20.5 14.5 %depthwise_project.1 = (bf16[512,768]{1,0:T(8,128)(2,1)S(1)}, bf16[512,768]{1,0:T(8,128)(2,1)S(1)}, bf16[768,2304]{1,0:T(8,128)(2,1)S(1)}, bf16[768,768]{1,0:T(8,128)(2,1)S(1)}) custom-call(s32[160,1]{1,0:T(8,128)} %constant.42.halo_order_ref, s32[512,1]{1,0:T(8,128)} %constant.43.fold_ref.natural_ref, s32[512,1]{1,0:T(8,128)} %constant.44.order_ref, ...), custom_call_target="tpu_custom_call" | custom-call | flops 4831838208 | bytes 9437184 | tf_op jit(solution)/shard_map/depthwise_project/pallas_call | solution.py:413
  35.0 25.6 %all_to_all.10 = bf16[32,2,1,1,8,768]{5,4,1,3,2,0:T(8,128)(2,1)S(1)} all-to-all(bf16[32,2,1,1,8,768]{5,4,1,3,2,0:T(8,128)(2,1)S(1)} %bitcast.19), channel_id=1, replica_groups=mesh['row'=4,'col'=8] {'row','col'}, dimensions={0} | all-to-all | bytes 1572864 | tf_op jit(solution)/shard_map/all_to_all | solution.py:637
  60.6 9.1 %grid_attention.1 = bf16[512,768]{1,0:T(8,128)(2,1)S(1)} custom-call(bf16[512,768]{1,0:T(8,128)(2,1)S(1)} %bitcast.20, s32[512,1]{1,0:T(8,128)} %constant.46.pick_ref, s32[512,1]{1,0:T(8,128)} %constant.47.place_ref, bf16[768,2304]{1,0:T(8,128)(2,1)S(1)} %get-tuple-element.29.qkv_weight_ref, f32[2304]{0:T(1024)} %qkv_bias_ref.1, ...), custom_call_target="tpu_custom_call" | custom-call | flops 3019898880 | bytes 8388608 | tf_op jit(solution)/shard_map/grid_attention/pallas_call | solution.py:516
  69.7 24.0 %all_to_all.11 = bf16[32,2,1,1,8,768]{5,4,1,3,2,0:T(8,128)(2,1)S(1)} all-to-all(bf16[32,2,1,1,8,768]{5,4,1,3,2,0:T(8,128)(2,1)S(1)} %bitcast.21), channel_id=1, replica_groups=mesh['row'=4,'col'=8] {'row','col'}, dimensions={0} | all-to-all | bytes 1572864 | tf_op jit(solution)/shard_map/all_to_all | solution.py:654
  93.6 0.2 convert_bitcast_fusion
  93.8 0.1 copy.26
  93.9 1.1 %fusion = bf16[8,64,768]{2,1,0:T(8,128)(2,1)} fusion(f32[8,64,768]{2,1,0:T(8,128)S(1)} %bitcast.23, bf16[8,64,768]{2,1,0:T(8,128)(2,1)S(1)} %bitcast.22), kind=kLoop, calls=%fused_computation.2 | loop fusion | flops 1179648 | bytes 3145728 | tf_op jit(solution)/shard_map/convert_element_type | solution.py:659
  (1 shorter events, 0.0 us)
Async XLA Ops:
  1.0 11.3 %collective-permute-start.1 = (bf16[64,768]{1,0:T(8,128)(2,1)S(1)}, bf16[64,768]{1,0:T(8,128)(2,1)S(1)}, u32[]{:S(2)}, u32[]{:S(2)}) collective-permute-start(bf16[64,768]{1,0:T(8,128)(2,1)S(1)} %get-tuple-element.31), channel_id=1, source_target_pairs={{8,16},{16,8},{9,17},{17,9},{10,18},{18,10},{11,19},{19,11},{12,20... | collective-permute-start | bytes 294920 | tf_op jit(solution)/shard_map/ppermute | solution.py:439
  1.6 10.7 %collective-permute-start = (bf16[64,768]{1,0:T(8,128)(2,1)S(1)}, bf16[64,768]{1,0:T(8,128)(2,1)S(1)}, u32[]{:S(2)}, u32[]{:S(2)}) collective-permute-start(bf16[64,768]{1,0:T(8,128)(2,1)S(1)} %get-tuple-element.32), channel_id=1, source_target_pairs={{0,8},{16,24},{8,0},{24,16},{1,9},{17,25},{9,1},{25,17},{2,10},{18... | collective-permute-start | bytes 294920 | tf_op jit(solution)/shard_map/ppermute | solution.py:439
  12.4 8.1 %collective-permute-start.3 = (bf16[16,768]{1,0:T(8,128)(2,1)S(1)}, bf16[16,768]{1,0:T(8,128)(2,1)S(1)}, u32[]{:S(2)}, u32[]{:S(2)}) collective-permute-start(bf16[16,768]{1,0:T(8,128)(2,1)S(1)} %get-tuple-element.23), channel_id=1, source_target_pairs={{1,2},{3,4},{5,6},{2,1},{4,3},{6,5},{9,10},{11,12},{13,14},{10,9},... | collective-permute-start | bytes 73736 | tf_op jit(solution)/shard_map/ppermute | solution.py:439
  13.0 7.5 %collective-permute-start.2 = (bf16[16,768]{1,0:T(8,128)(2,1)S(1)}, bf16[16,768]{1,0:T(8,128)(2,1)S(1)}, u32[]{:S(2)}, u32[]{:S(2)}) collective-permute-start(bf16[16,768]{1,0:T(8,128)(2,1)S(1)} %get-tuple-element.21._), channel_id=1, source_target_pairs={{0,1},{2,3},{4,5},{6,7},{1,0},{3,2},{5,4},{7,6},{8,9},{10,11},{12,... | collective-permute-start | bytes 73736 | tf_op jit(solution)/shard_map/ppermute | solution.py:439

commit v3 on v2

--- a/solution.py
+++ b/solution.py
@@ -14,6 +14,7 @@
 GRID = 8
 LANES = 128
 PACK = LANES // HEAD_DIM
+TOGETHER = 2
 
 
 def gelu(v):
@@ -43,13 +44,10 @@
 FOLD = 8
 
 
-def one_hot(index_ref, count):
-    column = lax.broadcasted_iota(jnp.int32, (index_ref.shape[0], count), 1)
-    return (column == index_ref[...]).astype(jnp.float32).astype(jnp.bfloat16)
-
-
-def shuffled(index_ref, values):
-    pick = one_hot(index_ref, values.shape[0])
+def shuffled(target_ref, values, count=None):
+    shape = (count or values.shape[0], values.shape[0])
+    row = lax.broadcasted_iota(jnp.int32, shape, 0)
+    pick = (row == target_ref[...]).astype(jnp.float32).astype(jnp.bfloat16)
     return jnp.dot(pick, values, preferred_element_type=jnp.float32).astype(jnp.bfloat16)
 
 
@@ -62,6 +60,8 @@
 
 INSIDE = pl.BlockSpec(memory_space=pltpu.VMEM)
 BLOCK = 256
+TWO = 2
+WIDE = TWO * BLOCK
 TALL = 128
 
 
@@ -86,77 +86,79 @@
     return (x.astype(jnp.float32) * row_of(scale_ref) + row_of(shift_ref)).astype(jnp.bfloat16)
 
 
-def expand_low_kernel(
-    x_ref,
-    fold_ref,
-    columns_ref,
-    scale_ref,
-    shift_ref,
-    bias_ref,
-    weight_ref,
-    o_ref,
-    folded_ref,
-    edges_ref,
-    held_ref,
-    normed_ref,
-    sems,
-):
+def expand_low_kernel(smalls, *refs):
+    x_ref, fold_ref, columns_ref, weight_ref, *refs = refs
+    sources, refs = refs[:smalls], refs[smalls:]
+    o_ref, folded_ref, edges_ref, held_ref, *refs = refs
+    targets, refs = refs[:smalls], refs[smalls:]
+    x_held_ref, fold_held_ref, columns_held_ref, normed_ref, sems, first_sems, small_sems = refs
+    firsts = [
+        pltpu.make_async_copy(source, target, first_sems.at[i])
+        for i, (source, target) in enumerate(
+            [
+                (x_ref, x_held_ref),
+                (fold_ref, fold_held_ref),
+                (columns_ref, columns_held_ref),
+            ]
+        )
+    ]
+    hand_on = [
+        pltpu.make_async_copy(source, target, small_sems.at[i])
+        for i, (source, target) in enumerate(zip(sources, targets, strict=True))
+    ]
     copies = fetch(weight_ref, held_ref, sems, 0, held_ref.shape[0])
-    for copy in copies:
+    needed = 3
+    for copy in firsts + hand_on[:needed] + copies + hand_on[needed:]:
         copy.start()
-    x = x_ref[...]
-    folded = shuffled(fold_ref, x)
+    for copy in firsts + hand_on[:needed]:
+        copy.wait()
+    scale_ref, shift_ref, bias_ref = targets[:needed]
+    x = x_held_ref[...]
+    folded = shuffled(fold_held_ref, x)
     folded_ref[...] = folded
-    edges_ref[...] = shuffled(columns_ref, x)
+    edges_ref[...] = shuffled(columns_held_ref, x, edges_ref.shape[0])
     normed_ref[...] = normalize(folded, scale_ref, shift_ref)
     expand_all(0, normed_ref, bias_ref, copies, held_ref, o_ref)
+    for copy in hand_on[needed:]:
+        copy.wait()
 
 
 def expand_high_kernel(
-    scale_ref,
-    shift_ref,
-    bias_ref,
-    folded_ref,
-    _,
-    weight_ref,
-    project_ref,
-    o_ref,
-    held_ref,
-    project_held_ref,
-    normed_ref,
-    sems,
-    project_sem,
+    scale_ref, shift_ref, bias_ref, folded_ref, _, weight_ref, o_ref, held_ref, normed_ref, sems
 ):
     steps = held_ref.shape[0]
     copies = fetch(weight_ref, held_ref, sems, steps, steps)
-    project = pltpu.make_async_copy(project_ref, project_held_ref, project_sem)
     for copy in copies:
         copy.start()
-    project.start()
     normed_ref[...] = normalize(folded_ref[...], scale_ref, shift_ref)
     expand_all(steps, normed_ref, bias_ref, copies, held_ref, o_ref)
-    project.wait()
-
-
-def expand_low(fold, columns, tokens, scale, shift, weight, bias):
+
+
+def expand_low(fold, columns, edge_count, tokens, weight, smalls):
     count, channels = tokens.shape
     width = weight.shape[1] // 2
     steps = width // BLOCK
-    smalls = [tokens, fold, columns, scale, shift, bias]
+    arrays = [tokens, fold, columns, weight, *smalls]
+    shapes = [
+        jax.ShapeDtypeStruct((count, width), jnp.float32),
+        jax.ShapeDtypeStruct((count, channels), jnp.bfloat16),
+        jax.ShapeDtypeStruct((edge_count, channels), jnp.bfloat16),
+        jax.ShapeDtypeStruct((steps, channels, BLOCK), jnp.bfloat16),
+        *like(*smalls),
+    ]
     return pl.pallas_call(
-        expand_low_kernel,
-        grid=(1,),
-        out_shape=[
-            jax.ShapeDtypeStruct((count, width), jnp.float32),
-            jax.ShapeDtypeStruct((count, channels), jnp.bfloat16),
-            jax.ShapeDtypeStruct((columns.shape[0], channels), jnp.bfloat16),
-            jax.ShapeDtypeStruct((steps, channels, BLOCK), jnp.bfloat16),
-        ],
-        in_specs=[whole(array) for array in smalls] + [OUTSIDE],
-        out_specs=[INSIDE] * 4,
+        functools.partial(expand_low_kernel, len(smalls)),
+        out_shape=shapes,
+        in_specs=[OUTSIDE] * len(arrays),
+        out_specs=[INSIDE] * len(shapes),
         scratch_shapes=[
+            pltpu.VMEM(tokens.shape, tokens.dtype),
+            pltpu.VMEM(fold.shape, fold.dtype),
+            pltpu.VMEM(columns.shape, columns.dtype),
             pltpu.VMEM((count, channels), jnp.bfloat16),
             pltpu.SemaphoreType.DMA((steps,)),
+            pltpu.SemaphoreType.DMA((3,)),
+            pltpu.SemaphoreType.DMA((len(smalls),)),
         ],
         cost_estimate=pl.CostEstimate(
             flops=2 * count * channels * width,
@@ -165,29 +167,24 @@
         ),
         compiler_params=pltpu.CompilerParams(vmem_limit_bytes=12 << 20),
         name="expand_low",
-    )(*[in_hbm(array) for array in smalls], in_hbm(weight))
-
-
-def expand_high(folded, after, scale, shift, weight, bias, project_weight):
+    )(*[in_hbm(array) for array in arrays])
+
+
+def expand_high(folded, after, scale, shift, weight, bias):
     count, channels = folded.shape
     width = weight.shape[1] // 2
     steps = width // BLOCK
-    smalls = [scale, shift, bias]
     return pl.pallas_call(
         expand_high_kernel,
-        grid=(1,),
         out_shape=[
             jax.ShapeDtypeStruct((count, width), jnp.float32),
             jax.ShapeDtypeStruct((steps, channels, BLOCK), jnp.bfloat16),
-            *like(project_weight),
         ],
-        in_specs=[whole(array) for array in smalls]
-        + [INSIDE, pl.BlockSpec(memory_space=pl.ANY), OUTSIDE, OUTSIDE],
-        out_specs=[INSIDE] * 3,
+        in_specs=[INSIDE] * 4 + [pl.BlockSpec(memory_space=pl.ANY), OUTSIDE],
+        out_specs=[INSIDE] * 2,
         scratch_shapes=[
             pltpu.VMEM((count, channels), jnp.bfloat16),
             pltpu.SemaphoreType.DMA((steps,)),
-            pltpu.SemaphoreType.DMA,
         ],
         cost_estimate=pl.CostEstimate(
             flops=2 * count * channels * width,
@@ -196,7 +193,7 @@
         ),
         compiler_params=pltpu.CompilerParams(vmem_limit_bytes=12 << 20),
         name="expand_high",
-    )(*[in_hbm(array) for array in smalls], folded, after, in_hbm(weight), in_hbm(project_weight))
+    )(scale, shift, bias, folded, after, in_hbm(weight))
 
 
 def edges_kernel(tall, first_row_ref, second_row_ref, edges_ref, first_ref, second_ref):
@@ -253,8 +250,8 @@
     second_col_ref,
     low_weight_ref,
     high_weight_ref,
+    features_ref,
     project_weight_ref,
-    features_ref,
     qkv_weight_ref,
     out_weight_ref,
     after_ref,
@@ -266,7 +263,10 @@
     left_ref,
     right_ref,
     depth_ref,
+    total_ref,
+    project_held_ref,
     sems,
+    project_sems,
 ):
     f32, bf16 = jnp.float32, jnp.bfloat16
     rows, cols = shape
@@ -277,6 +277,16 @@
         pltpu.make_async_copy(qkv_weight_ref, qkv_held_ref, sems.at[0]),
         pltpu.make_async_copy(out_weight_ref, out_held_ref, sems.at[1]),
     ]
+    half = low_weight_ref.shape[0] // TWO
+
+    def project_copy(step):
+        rows_at = pl.ds(pl.multiple_of(step * WIDE, WIDE), WIDE)
+        return pltpu.make_async_copy(
+            project_weight_ref.at[rows_at], project_held_ref.at[step], project_sems.at[step]
+        )
+
+    for step in range(2 * half):
+        project_copy(step).start()
     for copy in prefetch:
         copy.start()
 
@@ -312,36 +322,52 @@
     )
     normed_ref[...] = shuffled(halo_order_ref, normalize(halo, scale_ref, shift_ref))
 
+    depth_ref[1] = jnp.zeros_like(depth_ref[1])
+    total_ref[...] = features_ref[...].astype(f32) + row_of(project_bias_ref)
+
+    def add_chunk(at, slot):
+        total_ref[...] += jnp.dot(
+            depth_ref[slot], project_held_ref[at], preferred_element_type=f32
+        )
+
     def convolve(step, hidden_ref, weight_ref, offset):
+        slot = lax.rem(step + offset, 2)
+        project_copy(step + offset).wait()
+        add_chunk(jnp.maximum(step + offset - 1, 0), 1 - slot)
+        for sub in range(TWO):
+            convolve_block(step * TWO + sub, hidden_ref, weight_ref, offset * TWO, slot, sub)
+
+    def convolve_block(step, hidden_ref, weight_ref, offset, slot, sub):
         base = pl.multiple_of((step + offset) * BLOCK, BLOCK)
         part = jnp.dot(normed_ref[...], weight_ref[step], preferred_element_type=f32)
         bias = expand_bias_ref[pl.ds(base, BLOCK)].reshape(1, BLOCK)
-        halo_hidden_ref[...] = gelu(part + bias) * keep
+        halo_hidden_ref[sub] = gelu(part + bias) * keep
         for lane in range(BLOCK // LANES):
             lanes = slice(lane * LANES, (lane + 1) * LANES)
+            wide_lanes = slice(sub * BLOCK + lane * LANES, sub * BLOCK + (lane + 1) * LANES)
             inner = pl.ds(pl.multiple_of(step * BLOCK + lane * LANES, LANES), LANES)
             outer = pl.ds(pl.multiple_of(base + lane * LANES, LANES), LANES)
-            left = halo_hidden_ref[pl.ds(pl.multiple_of(left_at, 8), strip), lanes]
-            right = halo_hidden_ref[pl.ds(pl.multiple_of(right_at, 8), strip), lanes]
+            left = halo_hidden_ref[sub, pl.ds(pl.multiple_of(left_at, 8), strip), lanes]
+            right = halo_hidden_ref[sub, pl.ds(pl.multiple_of(right_at, 8), strip), lanes]
 
             def cell(r, j):
                 if r == 0 or r == tall - 1:
                     at = (top_at if r == 0 else bottom_at) + j * FOLD
-                    return halo_hidden_ref[pl.ds(pl.multiple_of(at, 8), FOLD), lanes]
+                    return halo_hidden_ref[sub, pl.ds(pl.multiple_of(at, 8), FOLD), lanes]
                 at = ((r - 1) * planes + j) * FOLD
                 return hidden_ref[at : at + FOLD, inner]
 
             for r in range(tall):
-                left_ref[lane, r, 8 : 8 + FOLD, :] = cell(r, planes - 1)
-                left_ref[lane, r, 7:8, :] = left[r : r + 1]
-                right_ref[lane, r, 0:FOLD, :] = cell(r, 0)
-                right_ref[lane, r, FOLD : FOLD + 1, :] = right[r : r + 1]
+                left_ref[BLOCK // LANES * sub + lane, r, 8 : 8 + FOLD, :] = cell(r, planes - 1)
+                left_ref[BLOCK // LANES * sub + lane, r, 7:8, :] = left[r : r + 1]
+                right_ref[BLOCK // LANES * sub + lane, r, 0:FOLD, :] = cell(r, 0)
+                right_ref[BLOCK // LANES * sub + lane, r, FOLD : FOLD + 1, :] = right[r : r + 1]
 
             def shifted(r, j):
                 if j < 0:
-                    return left_ref[lane, r, 7 : 7 + FOLD, :]
+                    return left_ref[BLOCK // LANES * sub + lane, r, 7 : 7 + FOLD, :]
                 if j == planes:
-                    return right_ref[lane, r, 1 : 1 + FOLD, :]
+                    return right_ref[BLOCK // LANES * sub + lane, r, 1 : 1 + FOLD, :]
                 return cell(r, j)
 
             taps = [
@@ -368,11 +394,9 @@
                     h = r - 2
                     if h >= 0:
                         lo = (h * planes + start) * FOLD
-                        depth_ref[lo : lo + pair * FOLD, outer] = jnp.concatenate(
+                        depth_ref[slot, lo : lo + pair * FOLD, wide_lanes] = jnp.concatenate(
                             [gelu(sums[k][h]) for k in range(pair)], axis=0
                         ).astype(bf16)
-
-    half = low_weight_ref.shape[0]
 
     def low_step(step, carry):
         convolve(step, low_ref, low_weight_ref, 0)
@@ -389,9 +413,10 @@
     normals, afters = [], []
     for lo in range(0, rows * cols, group):
         part = slice(lo, lo + group)
-        total = jnp.dot(depth_ref[part], project_weight_ref[...], preferred_element_type=f32)
-        after = features_ref[part].astype(f32) + total + row_of(project_bias_ref)
-        after = after.astype(bf16)
+        total = total_ref[part] + jnp.dot(
+            depth_ref[(2 * half - 1) % 2, part], project_held_ref[2 * half - 1], preferred_element_type=f32
+        )
+        after = total.astype(bf16)
         wide = after.astype(f32)
         center = wide - jnp.mean(wide, axis=-1, keepdims=True)
         spread = jnp.mean(center * center, axis=-1, keepdims=True)
@@ -404,25 +429,29 @@
         copy.wait()
 
 
-def convolve(shape, smalls, larges, qkv_weight, out_weight):
+def convolve(shape, smalls, larges, project_weight, qkv_weight, out_weight):
     rows, cols = shape
     features = larges[-1]
     count, channels = features.shape
     width = larges[0].shape[1] * 2
-    around = smalls[0].shape[0]
+    inputs = [*smalls, *larges]
+    steps = width // WIDE
+    around = smalls[0].shape[1]
     return pl.pallas_call(
         functools.partial(conv_kernel, shape),
-        grid=(1,),
         out_shape=like(features, features, qkv_weight, out_weight),
-        in_specs=[whole(array) for array in smalls] + [INSIDE] * len(larges) + [OUTSIDE] * 2,
+        in_specs=[INSIDE] * len(inputs) + [OUTSIDE] * 3,
         out_specs=[INSIDE] * 4,
         scratch_shapes=[
             pltpu.VMEM((around, channels), jnp.bfloat16),
-            pltpu.VMEM((around, BLOCK), jnp.float32),
-            pltpu.VMEM((BLOCK // LANES, rows + 2, FOLD + 8, LANES), jnp.float32),
-            pltpu.VMEM((BLOCK // LANES, rows + 2, FOLD + 8, LANES), jnp.float32),
-            pltpu.VMEM((count, width), jnp.bfloat16),
+            pltpu.VMEM((TWO, around, BLOCK), jnp.float32),
+            pltpu.VMEM((WIDE // LANES, rows + 2, FOLD + 8, LANES), jnp.float32),
+            pltpu.VMEM((WIDE // LANES, rows + 2, FOLD + 8, LANES), jnp.float32),
+            pltpu.VMEM((2, count, WIDE), jnp.bfloat16),
+            pltpu.VMEM((count, channels), jnp.float32),
+            pltpu.VMEM((steps, WIDE, channels), jnp.bfloat16),
             pltpu.SemaphoreType.DMA((2,)),
+            pltpu.SemaphoreType.DMA((steps,)),
         ],
         cost_estimate=pl.CostEstimate(
             flops=4 * count * channels * width,
@@ -431,7 +460,7 @@
         ),
         compiler_params=pltpu.CompilerParams(vmem_limit_bytes=24 << 20),
         name="depthwise_project",
-    )(*[in_hbm(array) for array in smalls], *larges, in_hbm(qkv_weight), in_hbm(out_weight))
+    )(*inputs, in_hbm(project_weight), in_hbm(qkv_weight), in_hbm(out_weight))
 
 
 def swap(cells, axis, count, odd_pairs):
@@ -473,7 +502,7 @@
     top = float(jnp.finfo(bf16).max)
     chunks = channels // LANES
 
-    def one_group(group, carry):
+    def one_group(group, probs_ref):
         rows = pl.ds(pl.multiple_of(group * group_size, group_size), group_size)
         for chunk in range(chunks):
             lo = chunk * LANES
@@ -496,33 +525,33 @@
                 values,
                 preferred_element_type=f32,
             ).astype(bf16)
+
+    together = probs_ref.shape[0]
+
+    def some_groups(at, carry):
+        for k in range(together):
+            one_group(at * together + k, probs_ref.at[k])
         return carry
 
-    lax.fori_loop(0, count // group_size, one_group, 0)
+    lax.fori_loop(0, count // group_size // together, some_groups, 0)
     result = jnp.dot(mixed_ref[...], out_weight_ref[...], preferred_element_type=f32)
     o_ref[...] = shuffled(place_ref, (result + row_of(out_bias_ref)).astype(bf16))
 
 
-def attend(tokens, order, group_size, qkv_weight, qkv_bias, out_weight, out_bias):
+def attend(tokens, pick, place, group_size, qkv_weight, qkv_bias, out_weight, out_bias):
     count, channels = tokens.shape
-    pick = np.asarray(order, np.int32)
-    place = np.argsort(pick).astype(np.int32)
-    inside = pl.BlockSpec(memory_space=pltpu.VMEM)
-    smalls = [jnp.asarray(pick)[:, None], jnp.asarray(place)[:, None], qkv_bias, out_bias]
-    pick, place, qkv_bias, out_bias = [in_hbm(array) for array in smalls]
     arrays = [tokens, pick, place, qkv_weight, qkv_bias, out_weight, out_bias]
-    specs = [whole(array) for array in arrays]
-    specs[0] = specs[3] = specs[5] = inside
     return pl.pallas_call(
         functools.partial(attend_kernel, group_size),
-        grid=(1,),
         out_shape=jax.ShapeDtypeStruct((count, channels), jnp.bfloat16),
-        in_specs=specs,
-        out_specs=inside,
+        in_specs=[INSIDE] * len(arrays),
+        out_specs=INSIDE,
         scratch_shapes=[
             pltpu.VMEM((count, 3 * channels), jnp.bfloat16),
             pltpu.VMEM((count, channels), jnp.bfloat16),
-            pltpu.VMEM((channels // LANES * group_size, PACK * group_size), jnp.float32),
+            pltpu.VMEM(
+                (TOGETHER, channels // LANES * group_size, PACK * group_size), jnp.float32
+            ),
         ],
         cost_estimate=pl.CostEstimate(
             flops=10 * count * channels * channels, bytes_accessed=8 << 20, transcendentals=1 << 20
@@ -564,29 +593,19 @@
     columns[0, 1 : tall - 1] = np.arange(tile_rows) * tile_cols
     columns[1, 1 : tall - 1] = np.arange(tile_rows) * tile_cols + tile_cols - 1
 
-    def index_array(values):
-        return jnp.asarray(np.asarray(values, np.int32).reshape(-1))[:, None]
+    def targets(sources, count):
+        sources = np.asarray(sources).reshape(-1)
+        found = np.full(count, -1, np.int32)
+        found[sources[sources >= 0]] = np.flatnonzero(sources >= 0)
+        return jnp.asarray(found)[None]
+
+    count = tile_rows * tile_cols
 
     row_even = row_at % 2 == 0
     near = lax.dynamic_slice_in_dim(features, jnp.where(row_even, tile_rows - 1, 0), 1, 0)[0]
     far = lax.dynamic_slice_in_dim(features, jnp.where(row_even, 0, tile_rows - 1), 1, 0)[0]
     first_row = swap(near, "row", row_count, False)
     second_row = swap(far, "row", row_count, True)
-    low, folded, edges, low_weight = expand_low(
-        index_array(fold),
-        index_array(columns),
-        flat,
-        norm_scale,
-        norm_shift,
-        expand_weight,
-        expand_bias,
-    )
-    first_col, second_col = edges_to_send(tall, first_row, second_row, edges)
-    high, high_weight, project_held = expand_high(
-        folded, first_col, norm_scale, norm_shift, expand_weight, expand_bias, project_weight
-    )
-    first_col = swap(first_col, "col", col_count, False)
-    second_col = swap(second_col, "col", col_count, True)
     fold_row = max(1, GRID // row_count)
     fold_col = max(1, GRID // col_count)
     parity_row = max(1, row_count // GRID)
@@ -600,21 +619,51 @@
     around = np.concatenate(
         [one_row, tile_cols + one_row, 2 * tile_cols + np.arange(2 * strip)]
     )
-    after_conv, ordered, qkv_weight, out_weight = convolve(
-        (tile_rows, tile_cols),
+    layout = np.arange(tile_rows * tile_cols).reshape(
+        row_count // parity_row,
+        parity_row,
+        col_count // parity_col,
+        parity_col,
+        fold_row,
+        block_row,
+        fold_col,
+        block_col,
+    )
+    pick = layout.transpose(1, 3, 5, 7, 0, 2, 4, 6)
+    group_size = math.prod(pick.shape[4:])
+    pick = pick.reshape(-1)
+    low, folded, edges, low_weight, *smalls = expand_low(
+        targets(fold, count),
+        targets(columns, count),
+        2 * strip,
+        flat,
+        expand_weight,
         [
-            index_array(around),
-            index_array(unfold),
-            index_array(unfold[source]),
             norm_scale,
             norm_shift,
             expand_bias,
+            targets(around, around.size),
+            targets(unfold, count),
+            targets(unfold[source], count),
             depth_kernel,
             depth_bias,
             project_bias,
             attn_gain,
             attn_shift,
+            targets(pick, count),
+            targets(np.argsort(pick), count),
+            qkv_bias,
+            out_bias,
         ],
+    )
+    scale, shift, bias = smalls[:3]
+    first_col, second_col = edges_to_send(tall, first_row, second_row, edges)
+    high, high_weight = expand_high(folded, first_col, scale, shift, expand_weight, bias)
+    first_col = swap(first_col, "col", col_count, False)
+    second_col = swap(second_col, "col", col_count, True)
+    after_conv, ordered, qkv_weight, out_weight = convolve(
+        (tile_rows, tile_cols),
+        [*smalls[3:5], smalls[5], scale, shift, bias, *smalls[6:11]],
         [
             low,
             high,
@@ -624,32 +673,21 @@
             second_col,
             low_weight,
             high_weight,
-            project_held,
             folded,
         ],
+        project_weight,
         qkv_weight,
         out_weight,
     )
+    pick, place, qkv_bias, out_bias = smalls[11:]
     after_conv = after_conv.reshape(features.shape)
     ordered = ordered.reshape(
         row_count * col_count, fold_row, block_row, fold_col, block_col, channels
     )
     received = lax.all_to_all(ordered, ("row", "col"), split_axis=0, concat_axis=0, tiled=True)
     tokens = received.reshape(-1, channels)
-    layout = np.arange(tokens.shape[0]).reshape(
-        row_count // parity_row,
-        parity_row,
-        col_count // parity_col,
-        parity_col,
-        fold_row,
-        block_row,
-        fold_col,
-        block_col,
-    )
-    order = layout.transpose(1, 3, 5, 7, 0, 2, 4, 6)
-    group_size = math.prod(order.shape[4:])
     answered = attend(
-        tokens, order.reshape(-1), group_size, qkv_weight, qkv_bias, out_weight, out_bias
+        tokens, pick, place, group_size, qkv_weight, qkv_bias, out_weight, out_bias
     ).reshape(received.shape)
     returned = lax.all_to_all(answered, ("row", "col"), split_axis=0, concat_axis=0, tiled=True)
     returned_tiles = returned.reshape(

time: 95.4 us -> 90.7 us (0.951)
  Pallas kernels: 32.9 us -> 28.5 us
    pallas_call x4, Pallas kernels: 32.9 us -> 28.5 us  [the longest x1 12.1 us: convolve(): pl.pallas_call(functools.partial(conv_kernel, shape), out_shape=like(feat...]
where the time goes in v3:
time: 90.7 us; the launch traced here: 90.5 us
  blocking collectives  49.4 us (54%)
  Pallas kernels  28.5 us (31%)
  starting transfers between devices  10.1 us (11%)
  other arithmetic  1.28 us (1%)
  local copies, waits for them, and re-layouts  1.08 us (1%)
    all_to_all x1, blocking collectives, per_device(): lax.all_to_all(ordered, ('row', 'col'), split_axis=0, concat_axis=0, tile...  25.5 us
    all_to_all x1, blocking collectives, per_device(): lax.all_to_all(answered, ('row', 'col'), split_axis=0, concat_axis=0, til...  24 us
    pallas_call x1, Pallas kernels, convolve(): pl.pallas_call(functools.partial(conv_kernel, shape), out_shape=like(feat...  12.1 us
    ppermute x4, starting transfers between devices, swap(): return lax.ppermute(cells, axis, pairs + [(j, i) for i, j in pairs])  10.1 us
    pallas_call x1, Pallas kernels, attend(): pl.pallas_call(functools.partial(attend_kernel, group_size), out_shape=ja...  7.4 us
    pallas_call x1, Pallas kernels, expand_low(): pl.pallas_call(functools.partial(expand_low_kernel, len(smalls)), out_sha...  5.26 us
    pallas_call x1, Pallas kernels, expand_high(): pl.pallas_call(expand_high_kernel, out_shape=[jax.ShapeDtypeStruct((count...  3.7 us
  transfers between devices with their start and end apart: 4, of which 0 were waited for; matrix products, arithmetic and copies ran while one was open for 0% of the time, Pallas kernels for 10%

profile of v3, /device:TPU:0, one launch (start us, length us, event | category | flops | bytes accessed | tf_op | source)
XLA Modules:
  0.0 90.5 jit_solution(13967500868450671168)
XLA Ops:
  0.0 1.0 %dynamic-slice_bitcast_fusion = (bf16[64,768]{1,0:T(8,128)(2,1)S(1)}, bf16[64,768]{1,0:T(8,128)(2,1)S(1)}) fusion(bf16[8,64,768]{2,1,0:T(8,128)(2,1)} %param.22, s32[]{:T(128)S(6)} %select_n.18, s32[]{:T(128)S(6)} %select_n.17), kind=kLoop, calls=%fused_computation.3 | loop fusion | bytes 393224 | tf_op jit(solution)/shard_map/squeeze | solution.py:606
  1.0 0.7 collective-permute-start.1
  1.6 5.8 %collective-permute-start = (bf16[64,768]{1,0:T(8,128)(2,1)S(1)}, bf16[64,768]{1,0:T(8,128)(2,1)S(1)}, u32[]{:S(2)}, u32[]{:S(2)}) collective-permute-start(bf16[64,768]{1,0:T(8,128)(2,1)S(1)} %get-tuple-element.60), channel_id=1, source_target_pairs={{0,8},{16,24},{8,0},{24,16},{1,9},{17,25},{9,1},{25,17},{2,10},{18... | collective-permute-start | bytes 294920 | tf_op jit(solution)/shard_map/ppermute | solution.py:468
  7.4 5.3 %expand_low.1 = (f32[512,1536]{1,0:T(8,128)S(1)}, bf16[512,768]{1,0:T(8,128)(2,1)S(1)}, bf16[32,768]{1,0:T(8,128)(2,1)S(1)}, bf16[6,768,256]{2,1,0:T(8,128)(2,1)...) custom-call(bf16[512,768]{1,0:T(8,128)(2,1)} %bitcast.25, ...), custom_call_target="tpu_custom_call" | custom-call | flops 1207959552 | bytes 2359296 | tf_op jit(solution)/shard_map/expand_low/pallas_call | solution.py:149
  12.7 0.0 collective-permute-done.1.second_row_ref
  12.7 0.0 collective-permute-done.first_row_ref
  12.7 0.7 collective-permute-start.3
  13.4 3.0 %collective-permute-start.2 = (bf16[16,768]{1,0:T(8,128)(2,1)S(1)}, bf16[16,768]{1,0:T(8,128)(2,1)S(1)}, u32[]{:S(2)}, u32[]{:S(2)}) collective-permute-start(bf16[16,768]{1,0:T(8,128)(2,1)S(1)} %get-tuple-element.46._), channel_id=1, source_target_pairs={{0,1},{2,3},{4,5},{6,7},{1,0},{3,2},{5,4},{7,6},{8,9},{10,11},{12,... | collective-permute-start | bytes 73736 | tf_op jit(solution)/shard_map/ppermute | solution.py:468
  16.4 3.7 %expand_high.1 = (f32[512,1536]{1,0:T(8,128)S(1)}, bf16[6,768,256]{2,1,0:T(8,128)(2,1)S(1)}) custom-call(f32[768]{0:T(1024)S(1)} %get-tuple-element.35.scale_ref, f32[768]{0:T(1024)S(1)} %get-tuple-element.36.shift_ref, f32[3072]{0:T(1024)S(1)} %get-tuple-element.37.bias_ref.expand_bias_ref, bf16[512,768]{1,0:T(8,128)(2,1)S(1)} %get-tuple-element.44.folded_ref.features_ref, ...), custom_call_target="tpu_custom_call" | custom-call | flops 1207959552 | bytes 7077888 | tf_op jit(solution)/shard_map/expand_high/pallas_call | solution.py:177
  20.1 0.0 collective-permute-done.3.second_col_ref
  20.1 0.0 collective-permute-done.2.first_col_ref
  20.1 12.1 %depthwise_project.1 = (bf16[512,768]{1,0:T(8,128)(2,1)S(1)}, bf16[512,768]{1,0:T(8,128)(2,1)S(1)}, bf16[768,2304]{1,0:T(8,128)(2,1)S(1)}, bf16[768,768]{1,0:T(8,128)(2,1)S(1)}) custom-call(s32[1,160]{1,0:T(1,128)S(1)} %get-tuple-element.32.halo_order_ref, s32[1,512]{1,0:T(1,128)S(1)} %get-tuple-element.33.natural_ref, ...), custom_call_target="tpu_custom_call" | custom-call | flops 4831838208 | bytes 9437184 | tf_op jit(solution)/shard_map/depthwise_project/pallas_call | solution.py:440
  32.2 25.5 %all_to_all.10 = bf16[32,2,1,1,8,768]{5,4,1,3,2,0:T(8,128)(2,1)S(1)} all-to-all(bf16[32,2,1,1,8,768]{5,4,1,3,2,0:T(8,128)(2,1)S(1)} %bitcast.19), channel_id=1, replica_groups=mesh['row'=4,'col'=8] {'row','col'}, dimensions={0} | all-to-all | bytes 1572864 | tf_op jit(solution)/shard_map/all_to_all | solution.py:687
  57.7 7.4 %grid_attention.1 = bf16[512,768]{1,0:T(8,128)(2,1)S(1)} custom-call(bf16[512,768]{1,0:T(8,128)(2,1)S(1)} %bitcast.20, s32[1,512]{1,0:T(1,128)S(1)} %get-tuple-element.53.pick_ref, s32[1,512]{1,0:T(1,128)S(1)} %get-tuple-element.54.place_ref, bf16[768,2304]{1,0:T(8,128)(2,1)S(1)} %get-tuple-element.55.qkv_weight_ref, ...), custom_call_target="tpu_custom_call" | custom-call | flops 3019898880 | bytes 8388608 | tf_op jit(solution)/shard_map/grid_attention/pallas_call | solution.py:544
  65.1 24.0 %all_to_all.11 = bf16[32,2,1,1,8,768]{5,4,1,3,2,0:T(8,128)(2,1)S(1)} all-to-all(bf16[32,2,1,1,8,768]{5,4,1,3,2,0:T(8,128)(2,1)S(1)} %bitcast.21), channel_id=1, replica_groups=mesh['row'=4,'col'=8] {'row','col'}, dimensions={0} | all-to-all | bytes 1572864 | tf_op jit(solution)/shard_map/all_to_all | solution.py:692
  89.1 0.2 convert_bitcast_fusion
  89.3 0.1 copy.26
  89.4 1.1 %fusion = bf16[8,64,768]{2,1,0:T(8,128)(2,1)} fusion(f32[8,64,768]{2,1,0:T(8,128)S(1)} %bitcast.23, bf16[8,64,768]{2,1,0:T(8,128)(2,1)S(1)} %bitcast.22), kind=kLoop, calls=%fused_computation.2 | loop fusion | flops 1179648 | bytes 3145728 | tf_op jit(solution)/shard_map/convert_element_type | solution.py:697
  (1 shorter events, 0.0 us)
Async XLA Ops:
  1.0 11.7 %collective-permute-start.1 = (bf16[64,768]{1,0:T(8,128)(2,1)S(1)}, bf16[64,768]{1,0:T(8,128)(2,1)S(1)}, u32[]{:S(2)}, u32[]{:S(2)}) collective-permute-start(bf16[64,768]{1,0:T(8,128)(2,1)S(1)} %get-tuple-element.59), channel_id=1, source_target_pairs={{8,16},{16,8},{9,17},{17,9},{10,18},{18,10},{11,19},{19,11},{12,20... | collective-permute-start | bytes 294920 | tf_op jit(solution)/shard_map/ppermute | solution.py:468
  1.6 11.1 %collective-permute-start = (bf16[64,768]{1,0:T(8,128)(2,1)S(1)}, bf16[64,768]{1,0:T(8,128)(2,1)S(1)}, u32[]{:S(2)}, u32[]{:S(2)}) collective-permute-start(bf16[64,768]{1,0:T(8,128)(2,1)S(1)} %get-tuple-element.60), channel_id=1, source_target_pairs={{0,8},{16,24},{8,0},{24,16},{1,9},{17,25},{9,1},{25,17},{2,10},{18... | collective-permute-start | bytes 294920 | tf_op jit(solution)/shard_map/ppermute | solution.py:468
  12.7 7.4 %collective-permute-start.3 = (bf16[16,768]{1,0:T(8,128)(2,1)S(1)}, bf16[16,768]{1,0:T(8,128)(2,1)S(1)}, u32[]{:S(2)}, u32[]{:S(2)}) collective-permute-start(bf16[16,768]{1,0:T(8,128)(2,1)S(1)} %get-tuple-element.48), channel_id=1, source_target_pairs={{1,2},{3,4},{5,6},{2,1},{4,3},{6,5},{9,10},{11,12},{13,14},{10,9},... | collective-permute-start | bytes 73736 | tf_op jit(solution)/shard_map/ppermute | solution.py:468
  13.4 6.7 %collective-permute-start.2 = (bf16[16,768]{1,0:T(8,128)(2,1)S(1)}, bf16[16,768]{1,0:T(8,128)(2,1)S(1)}, u32[]{:S(2)}, u32[]{:S(2)}) collective-permute-start(bf16[16,768]{1,0:T(8,128)(2,1)S(1)} %get-tuple-element.46._), channel_id=1, source_target_pairs={{0,1},{2,3},{4,5},{6,7},{1,0},{3,2},{5,4},{7,6},{8,9},{10,11},{12,... | collective-permute-start | bytes 73736 | tf_op jit(solution)/shard_map/ppermute | solution.py:468
